TPU v7x, 16 devices: a whole 2x2x2 slice. The times are simulated.
16 devices in a mesh: data: 2 (over z), expert: 8 (over y, x, core).
Axes of the slice: x: 2, y: 2, z: 2, core: 2. Of those that a mesh axis runs over, the one named last changes fastest.
Arguments:
- x_tokens: bfloat16 [1024, 1024], P(('data', 'expert')), parts along dimension 0
- y_mid: bfloat16 [1024, 1024], P(('data', 'expert')), parts along dimension 0
- dy_out: bfloat16 [1024, 1024], P(('data', 'expert')), parts along dimension 0
- experts_one: int32 [1024, 8], P(('data', 'expert')), parts along dimension 0
- gates_one: float32 [1024, 8], P(('data', 'expert')), parts along dimension 0
- slots_one: int32 [1024, 8], P(('data', 'expert')), parts along dimension 0
- experts_two: int32 [1024, 8], P(('data', 'expert')), parts along dimension 0
- gates_two: float32 [1024, 8], P(('data', 'expert')), parts along dimension 0
- slots_two: int32 [1024, 8], P(('data', 'expert')), parts along dimension 0
- w_gate_one: bfloat16 [32, 1024, 512], P('expert')
- w_up_one: bfloat16 [32, 1024, 512], P('expert')
- w_down_one: bfloat16 [32, 512, 1024], P('expert')
- w_gate_two: bfloat16 [32, 1024, 512], P('expert')
- w_up_two: bfloat16 [32, 1024, 512], P('expert')
- w_down_two: bfloat16 [32, 512, 1024], P('expert')
Outputs:
- output 1: bfloat16 [1024, 1024], P(('data', 'expert')), parts along dimension 0
- output 2: float32 [64, 1024, 512], P(('data', 'expert')), parts along dimension 0
- output 3: float32 [64, 1024, 512], P(('data', 'expert')), parts along dimension 0
- output 4: float32 [64, 512, 1024], P(('data', 'expert')), parts along dimension 0
- output 5: float32 [64, 1024, 512], P(('data', 'expert')), parts along dimension 0
- output 6: float32 [64, 1024, 512], P(('data', 'expert')), parts along dimension 0
- output 7: float32 [64, 512, 1024], P(('data', 'expert')), parts along dimension 0
There are 2 independent parts. A program takes and returns all parts, laid end to end along the dimension named above; an argument that names none is the same for every part.
All inputs are finite; a program needn't handle non-finite values.
Results may differ from a plain program's by a relative error of at most 0.01323.
Values are sent between devices in bfloat16 or wider.
A program may use at most 1 GiB of HBM per device.

v0:
```python
import functools
import jax
import jax.numpy as jnp
from jax import lax
from jax.sharding import PartitionSpec as P


def slot_capacity(tokens_dev, top_k, n_experts):
    return 8 * ((3 * top_k * tokens_dev + 16 * n_experts - 1) // (16 * n_experts))


def route_matrix(experts, slots, gates, n_experts, capacity):
    target = jnp.where(slots >= 0, experts * capacity + slots, -1)
    slot_ids = lax.broadcasted_iota(jnp.int32, (n_experts * capacity, 1), 0)
    matches = [slot_ids == target[None, :, choice] for choice in range(experts.shape[1])]
    send_mat = functools.reduce(jnp.logical_or, matches).astype(jnp.bfloat16)
    gate_terms = [jnp.sum(jnp.where(matches[choice], gates[None, :, choice], 0.0), axis=1) for choice in range(experts.shape[1])]
    return send_mat, functools.reduce(jnp.add, gate_terms)


def expert_grads(x_rows, dz_rows, w_gate, w_up, w_down):
    gate_act = jnp.einsum("erd,edf->erf", x_rows, w_gate, preferred_element_type=jnp.float32).astype(jnp.bfloat16)
    up_act = jnp.einsum("erd,edf->erf", x_rows, w_up, preferred_element_type=jnp.float32).astype(jnp.bfloat16)
    gate_wide = gate_act.astype(jnp.float32)
    up_wide = up_act.astype(jnp.float32)
    sig_gate = jax.nn.sigmoid(gate_wide)
    silu_gate = gate_wide * sig_gate
    hidden = (silu_gate * up_wide).astype(jnp.bfloat16)
    d_hidden = jnp.einsum("erd,efd->erf", dz_rows, w_down, preferred_element_type=jnp.float32)
    dw_down = jnp.einsum("erf,erd->efd", hidden, dz_rows, preferred_element_type=jnp.float32)
    d_gate = (d_hidden * up_wide * sig_gate * (1.0 + gate_wide * (1.0 - sig_gate))).astype(jnp.bfloat16)
    d_up = (d_hidden * silu_gate).astype(jnp.bfloat16)
    dx_rows = (jnp.einsum("erf,edf->erd", d_gate, w_gate, preferred_element_type=jnp.float32) + jnp.einsum("erf,edf->erd", d_up, w_up, preferred_element_type=jnp.float32)).astype(jnp.bfloat16)
    dw_gate = jnp.einsum("erd,erf->edf", x_rows, d_gate, preferred_element_type=jnp.float32)
    dw_up = jnp.einsum("erd,erf->edf", x_rows, d_up, preferred_element_type=jnp.float32)
    return dx_rows, dw_gate, dw_up, dw_down


def layer_backward(inputs, cotangent, experts, gates, slots, w_gate, w_up, w_down, group_size):
    tokens_dev, model_dim = inputs.shape
    n_experts = w_gate.shape[0] * group_size
    capacity = slot_capacity(tokens_dev, experts.shape[1], n_experts)
    send_mat, slot_gate = route_matrix(experts, slots, gates, n_experts, capacity)
    x_send = jnp.dot(send_mat, inputs, preferred_element_type=jnp.float32).astype(jnp.bfloat16)
    dy_send = jnp.dot(send_mat, cotangent, preferred_element_type=jnp.float32)
    z_send = (slot_gate[:, None] * dy_send).astype(jnp.bfloat16)
    x_rows = lax.all_to_all(x_send.reshape(n_experts, capacity, model_dim), "expert", 0, 1, tiled=True)
    dz_rows = lax.all_to_all(z_send.reshape(n_experts, capacity, model_dim), "expert", 0, 1, tiled=True)
    dx_rows, dw_gate, dw_up, dw_down = expert_grads(x_rows, dz_rows, w_gate, w_up, w_down)
    returned = lax.all_to_all(dx_rows, "expert", 1, 0, tiled=True).reshape(n_experts * capacity, model_dim)
    summed = jnp.einsum("rt,rd->td", send_mat, returned, preferred_element_type=jnp.float32)
    return summed, dw_gate, dw_up, dw_down


def solution(mesh):
    group_size = mesh.shape["expert"]
    tok_spec = P(("data", "expert"), None)
    weight_spec = P("expert", None, None)
    grad_spec = P(("data", "expert"), None, None)

    def local_step(x_tokens, y_mid, dy_out, experts_one, gates_one, slots_one, experts_two, gates_two, slots_two, w_gate_one, w_up_one, w_down_one, w_gate_two, w_up_two, w_down_two):
        grads_two = layer_backward(y_mid, dy_out, experts_two, gates_two, slots_two, w_gate_two, w_up_two, w_down_two, group_size)
        dy_mid = (dy_out.astype(jnp.float32) + grads_two[0]).astype(jnp.bfloat16)
        grads_one = layer_backward(x_tokens, dy_mid, experts_one, gates_one, slots_one, w_gate_one, w_up_one, w_down_one, group_size)
        dx_tokens = (dy_mid.astype(jnp.float32) + grads_one[0]).astype(jnp.bfloat16)
        return (dx_tokens,) + grads_one[1:] + grads_two[1:]

    return jax.shard_map(local_step, mesh=mesh, in_specs=(tok_spec,) * 9 + (weight_spec,) * 6, out_specs=(tok_spec,) + (grad_spec,) * 6, check_vma=False)
```

profile of v0, /device:TPU:0, one launch (start us, length us, event | category | flops | bytes accessed | tf_op | source)
XLA Modules:
  0.0 181.4 jit_solution(7177465843359892575)
XLA Ops:
  2.9 2.8 %multiply_convert_fusion.1 = bf16[768,1024]{1,0:T(8,128)(2,1)} fusion(bf16[64,1024]{1,0:T(8,128)(2,1)} %param.17, f32[768]{0:T(1024)S(1)} %add_add_fusion.1, s32[64]{0:T(128)S(1)} %get-tuple-element.24, s32[64]{0:T(128)S(1)} %get-tuple-element.25, s32[64]{0:T(128)S(1)} %get-tuple-element.26, s32[64]{0:T(128)S(1)} %get-tuple-element.27, ...), kind=kOutput, calls=%fused_computation.3 | convolution fusion | flops 102973440 | bytes 1709056 | tf_op jit(solution)/shard_map/dot_general | solution.py:45
  5.7 5.5 %all-to-all-start = ((bf16[32,24,1024]{2,1,0:T(8,128)(2,1)}), bf16[32,24,1024]{2,1,0:T(8,128)(2,1)S(1)}, u32[]{:S(2)}, u32[]{:S(2)}) async-start(bf16[32,24,1024]{2,1,0:T(8,128)(2,1)} %bitcast.16), calls=%async_computation | async-start | bytes 3145728 | tf_op jit(solution)/shard_map/all_to_all | solution.py:48
  11.2 1.9 %convolution_convert_fusion.1 = bf16[768,1024]{1,0:T(8,128)(2,1)} fusion(bf16[64,1024]{1,0:T(8,128)(2,1)S(1)} %copy-done, s32[64]{0:T(128)S(1)} %get-tuple-element.24, s32[64]{0:T(128)S(1)} %get-tuple-element.25, s32[64]{0:T(128)S(1)} %get-tuple-element.26, s32[64]{0:T(128)S(1)} %get-tuple-element.27, s32[64]{0:T(128)S(1)} %get-tuple-element.28, ...), kind=kOutput, calls=%fused_computation.15 | convolution fusion | flops 102187008 | bytes 1705984 | tf_op jit(solution)/shard_map/dot_general | solution.py:44
  13.1 19.1 %all-to-all-done = bf16[32,24,1024]{2,1,0:T(8,128)(2,1)S(1)} async-done(((bf16[32,24,1024]{2,1,0:T(8,128)(2,1)}), bf16[32,24,1024]{2,1,0:T(8,128)(2,1)S(1)}, u32[]{:S(2)}, u32[]{:S(2)}) %all-to-all-start) | async-done | bytes 1572896 | tf_op jit(solution)/shard_map/all_to_all | solution.py:48
  33.3 3.6 %all-to-all-start.1 = ((bf16[32,24,1024]{2,1,0:T(8,128)(2,1)}), bf16[32,24,1024]{2,1,0:T(8,128)(2,1)S(1)}, u32[]{:S(2)}, u32[]{:S(2)}) async-start(bf16[32,24,1024]{2,1,0:T(8,128)(2,1)} %bitcast.138), calls=%async_computation.1 | async-start | bytes 3145728 | tf_op jit(solution)/shard_map/all_to_all | solution.py:47
  37.2 1.9 %convolution_convert_fusion = bf16[768,1024]{1,0:T(8,128)(2,1)} fusion(bf16[64,1024]{1,0:T(8,128)(2,1)S(1)} %copy-done.26, s32[64]{0:T(128)S(1)} %get-tuple-element.8, s32[64]{0:T(128)S(1)} %get-tuple-element.9, s32[64]{0:T(128)S(1)} %get-tuple-element.10, s32[64]{0:T(128)S(1)} %get-tuple-element.11, s32[64]{0:T(128)S(1)} %get-tuple-element.12, ...), kind=kOutput, calls=%fused_computation.14 | convolution fusion | flops 102187008 | bytes 1705984 | tf_op jit(solution)/shard_map/dot_general | solution.py:44
  39.3 18.5 %all-to-all-done.1 = bf16[32,24,1024]{2,1,0:T(8,128)(2,1)S(1)} async-done(((bf16[32,24,1024]{2,1,0:T(8,128)(2,1)}), bf16[32,24,1024]{2,1,0:T(8,128)(2,1)S(1)}, u32[]{:S(2)}, u32[]{:S(2)}) %all-to-all-start.1) | async-done | bytes 1572896 | tf_op jit(solution)/shard_map/all_to_all | solution.py:47
  58.9 4.3 %all-to-all-start.4 = ((bf16[32,24,1024]{2,1,0:T(8,128)(2,1)}), bf16[32,24,1024]{2,1,0:T(8,128)(2,1)}, u32[]{:S(2)}, u32[]{:S(2)}) async-start(bf16[32,24,1024]{2,1,0:T(8,128)(2,1)} %bitcast.139), calls=%async_computation.4 | async-start | bytes 3145728 | tf_op jit(solution)/shard_map/all_to_all | solution.py:47
  64.8 3.3 %convolution_convert_fusion.4 = bf16[4,192,512]{2,1,0:T(8,128)(2,1)S(1)} fusion(bf16[4,192,1024]{2,1,0:T(8,128)(2,1)S(1)} %bitcast.124, bf16[4,1024,512]{2,1,0:T(8,128)(2,1)} %param.27), kind=kOutput, calls=%fused_computation.36 | convolution fusion | flops 805699584 | bytes 6553600 | tf_op jit(solution)/shard_map/erd,edf->erf/dot_general | solution.py:22
  69.3 1.7 copy-done.30
  71.0 1.8 %fusion.2 = (bf16[4,192,512]{2,1,0:T(8,128)(2,1)S(1)}, f32[4,192,512]{2,1,0:T(8,128)S(1)}) fusion(bf16[4,192,512]{2,1,0:T(8,128)(2,1)S(1)} %convolution_convert_fusion.5, bf16[4,192,512]{2,1,0:T(8,128)(2,1)S(1)} %convolution_convert_fusion.4, bf16[4,192,1024]{2,1,0:T(8,128)(2,1)S(1)} %bitcast.132, bf16[4,512,1024]{2,1,0:T(8,128)(2,1)S(1)} %copy-done.30), kind=kOutput, calls=%fused_computation.18 | convolution fusion | flops 810024960 | bytes 9699328 | tf_op jit(solution)/shard_map/erd,efd->erf/dot_general | solution.py:29
  76.3 2.4 %copy.50 = bf16[4,192,1024]{2,0,1:T(4,128)(2,1)} copy(bf16[4,192,1024]{2,1,0:T(8,128)(2,1)S(1)} %add_convert_fusion.1) | data formatting | bytes 3145728 | tf_op jit(solution)/shard_map/convert_element_type | solution.py:33
  78.6 5.5 %all-to-all-done.4 = bf16[32,24,1024]{2,1,0:T(8,128)(2,1)} async-done(((bf16[32,24,1024]{2,1,0:T(8,128)(2,1)}), bf16[32,24,1024]{2,1,0:T(8,128)(2,1)}, u32[]{:S(2)}, u32[]{:S(2)}) %all-to-all-start.4) | async-done | bytes 1572896 | tf_op jit(solution)/shard_map/all_to_all | solution.py:47
  84.1 4.5 %all-to-all-start.2 = ((bf16[4,192,1024]{2,0,1:T(4,128)(2,1)}), bf16[4,192,1024]{2,0,1:T(4,128)(2,1)}, u32[]{:S(2)}, u32[]{:S(2)}) async-start(bf16[4,192,1024]{2,0,1:T(4,128)(2,1)} %copy.50), calls=%async_computation.2 | async-start | bytes 3145728 | tf_op jit(solution)/shard_map/all_to_all | solution.py:50
  90.4 4.1 %convolution_convert_fusion.2 = bf16[4,192,512]{2,1,0:T(8,128)(2,1)} fusion(bf16[4,192,1024]{2,1,0:T(8,128)(2,1)S(1)} %bitcast.128, bf16[4,1024,512]{2,1,0:T(8,128)(2,1)} %param.24), kind=kOutput, calls=%fused_computation.34 | convolution fusion | flops 805699584 | bytes 6553600 | tf_op jit(solution)/shard_map/erd,edf->erf/dot_general | solution.py:22
  94.6 4.8 %fusion.49 = f32[4,1024,512]{2,1,0:T(8,128)} fusion(bf16[4,192,1024]{2,1,0:T(8,128)(2,1)S(1)} %bitcast.126, bf16[4,192,512]{2,1,0:T(8,128)(2,1)S(1)} %copy-done.20), kind=kOutput, calls=%fused_computation.133 | convolution fusion | flops 805306368 | bytes 10747904 | tf_op jit(solution)/shard_map/erd,erf->edf/dot_general | solution.py:34
  99.3 9.9 %all-to-all-done.2 = bf16[4,192,1024]{2,0,1:T(4,128)(2,1)} async-done(((bf16[4,192,1024]{2,0,1:T(4,128)(2,1)}), bf16[4,192,1024]{2,0,1:T(4,128)(2,1)}, u32[]{:S(2)}, u32[]{:S(2)}) %all-to-all-start.2) | async-done | bytes 1572896 | tf_op jit(solution)/shard_map/all_to_all | solution.py:50
  109.3 1.9 %copy.51 = bf16[4,192,1024]{2,1,0:T(8,128)(2,1)S(1)} copy(bf16[4,192,1024]{2,0,1:T(4,128)(2,1)} %all-to-all-done.2) | data formatting | bytes 3145728 | tf_op jit(solution)/shard_map/all_to_all | solution.py:50
  112.6 1.9 %multiply_convert_fusion = bf16[768,1024]{1,0:T(8,128)(2,1)} fusion(bf16[64,1024]{1,0:T(8,128)(2,1)S(1)} %fusion.16, f32[768]{0:T(1024)S(1)} %add_add_fusion, s32[64]{0:T(128)S(1)} %get-tuple-element.8, s32[64]{0:T(128)S(1)} %get-tuple-element.9, s32[64]{0:T(128)S(1)} %get-tuple-element.10, s32[64]{0:T(128)S(1)} %get-tuple-element.11, ...), kind=kOutput, calls=%fused_computation.1 | convolution fusion | flops 102973440 | bytes 1709056 | tf_op jit(solution)/shard_map/dot_general | solution.py:45
  114.5 4.3 %all-to-all-start.3 = ((bf16[32,24,1024]{2,1,0:T(8,128)(2,1)}), bf16[32,24,1024]{2,1,0:T(8,128)(2,1)}, u32[]{:S(2)}, u32[]{:S(2)}) async-start(bf16[32,24,1024]{2,1,0:T(8,128)(2,1)} %bitcast.142), calls=%async_computation.3 | async-start | bytes 3145728 | tf_op jit(solution)/shard_map/all_to_all | solution.py:48
  118.8 4.2 %convolution_convert_fusion.3 = bf16[4,192,512]{2,1,0:T(8,128)(2,1)} fusion(bf16[4,192,1024]{2,1,0:T(8,128)(2,1)S(1)} %bitcast.129, bf16[4,1024,512]{2,1,0:T(8,128)(2,1)} %param.25), kind=kOutput, calls=%fused_computation.35 | convolution fusion | flops 805699584 | bytes 6553600 | tf_op jit(solution)/shard_map/erd,edf->erf/dot_general | solution.py:23
  123.1 4.8 %fusion.20 = f32[4,512,1024]{2,1,0:T(8,128)} fusion(bf16[4,192,1024]{2,1,0:T(8,128)(2,1)S(1)} %bitcast.133, bf16[4,192,512]{2,1,0:T(8,128)(2,1)S(1)} %copy-done.14, bf16[4,192,512]{2,1,0:T(8,128)(2,1)S(1)} %copy-done.5), kind=kOutput, calls=%fused_computation.43 | convolution fusion | flops 808452096 | bytes 11534336 | tf_op jit(solution)/shard_map/erf,erd->efd/dot_general | solution.py:30
  127.8 4.8 %fusion.44 = f32[4,1024,512]{2,1,0:T(8,128)} fusion(bf16[4,192,1024]{2,1,0:T(8,128)(2,1)S(1)} %bitcast.127, f32[4,192,512]{2,1,0:T(8,128)S(1)} %copy-done.23, bf16[4,192,512]{2,1,0:T(8,128)(2,1)S(1)} %copy-done.5), kind=kOutput, calls=%fused_computation.128 | convolution fusion | flops 808058880 | bytes 12320768 | tf_op jit(solution)/shard_map/erd,erf->edf/dot_general | solution.py:35
  132.6 7.1 %all-to-all-done.3 = bf16[32,24,1024]{2,1,0:T(8,128)(2,1)} async-done(((bf16[32,24,1024]{2,1,0:T(8,128)(2,1)}), bf16[32,24,1024]{2,1,0:T(8,128)(2,1)}, u32[]{:S(2)}, u32[]{:S(2)}) %all-to-all-start.3) | async-done | bytes 1572896 | tf_op jit(solution)/shard_map/all_to_all | solution.py:48
  141.5 4.4 %fusion.6 = (bf16[4,192,512]{2,1,0:T(8,128)(2,1)S(1)}, f32[4,192,512]{2,1,0:T(8,128)S(1)}) fusion(bf16[4,192,512]{2,1,0:T(8,128)(2,1)S(1)} %copy-done.15, bf16[4,192,512]{2,1,0:T(8,128)(2,1)S(1)} %copy-done.6, bf16[4,192,1024]{2,1,0:T(8,128)(2,1)S(1)} %bitcast.134, bf16[4,512,1024]{2,1,0:T(8,128)(2,1)} %param.26), kind=kOutput, calls=%fused_computation.22 | convolution fusion | flops 810024960 | bytes 9699328 | tf_op jit(solution)/shard_map/erd,efd->erf/dot_general | solution.py:29
  150.6 2.4 %copy.55 = bf16[4,192,1024]{2,0,1:T(4,128)(2,1)} copy(bf16[4,192,1024]{2,1,0:T(8,128)(2,1)S(1)} %add_convert_fusion) | data formatting | bytes 3145728 | tf_op jit(solution)/shard_map/convert_element_type | solution.py:33
  153.0 4.5 %all-to-all-start.5 = ((bf16[4,192,1024]{2,0,1:T(4,128)(2,1)}), bf16[4,192,1024]{2,0,1:T(4,128)(2,1)}, u32[]{:S(2)}, u32[]{:S(2)}) async-start(bf16[4,192,1024]{2,0,1:T(4,128)(2,1)} %copy.55), calls=%async_computation.5 | async-start | bytes 3145728 | tf_op jit(solution)/shard_map/all_to_all | solution.py:50
  157.5 6.0 %fusion.48 = f32[4,1024,512]{2,1,0:T(8,128)} fusion(bf16[4,192,1024]{2,1,0:T(8,128)(2,1)S(1)} %bitcast.130, bf16[4,192,512]{2,1,0:T(8,128)(2,1)} %copy-done.21), kind=kOutput, calls=%fused_computation.132 | convolution fusion | flops 805306368 | bytes 10747904 | tf_op jit(solution)/shard_map/erd,erf->edf/dot_general | solution.py:34
  163.5 4.7 %fusion.18 = f32[4,512,1024]{2,1,0:T(8,128)} fusion(bf16[4,192,1024]{2,1,0:T(8,128)(2,1)S(1)} %bitcast.135, bf16[4,192,512]{2,1,0:T(8,128)(2,1)S(1)} %copy-done.15, bf16[4,192,512]{2,1,0:T(8,128)(2,1)S(1)} %copy-done.6), kind=kOutput, calls=%fused_computation.42 | convolution fusion | flops 808452096 | bytes 11534336 | tf_op jit(solution)/shard_map/erf,erd->efd/dot_general | solution.py:30
  168.3 4.8 %fusion.45 = f32[4,1024,512]{2,1,0:T(8,128)} fusion(bf16[4,192,1024]{2,1,0:T(8,128)(2,1)S(1)} %bitcast.131, f32[4,192,512]{2,1,0:T(8,128)S(1)} %copy-done.25, bf16[4,192,512]{2,1,0:T(8,128)(2,1)S(1)} %copy-done.6), kind=kOutput, calls=%fused_computation.129 | convolution fusion | flops 808058880 | bytes 12320768 | tf_op jit(solution)/shard_map/erd,erf->edf/dot_general | solution.py:35
  173.0 5.1 %all-to-all-done.5 = bf16[4,192,1024]{2,0,1:T(4,128)(2,1)} async-done(((bf16[4,192,1024]{2,0,1:T(4,128)(2,1)}), bf16[4,192,1024]{2,0,1:T(4,128)(2,1)}, u32[]{:S(2)}, u32[]{:S(2)}) %all-to-all-start.5) | async-done | bytes 1572896 | tf_op jit(solution)/shard_map/all_to_all | solution.py:50
  178.2 1.9 %copy.56 = bf16[4,192,1024]{2,1,0:T(8,128)(2,1)S(1)} copy(bf16[4,192,1024]{2,0,1:T(4,128)(2,1)} %all-to-all-done.5) | data formatting | bytes 3145728 | tf_op jit(solution)/shard_map/all_to_all | solution.py:50
  (92 shorter events, 22.0 us)
Async XLA Ops:
  0.6 10.5 %copy-start = (bf16[64,1024]{1,0:T(8,128)(2,1)S(1)}, bf16[64,1024]{1,0:T(8,128)(2,1)}, u32[]{:S(2)}) copy-start(bf16[64,1024]{1,0:T(8,128)(2,1)} %param.16) | copy-start | bytes 393220
  5.7 26.4 %all-to-all-start = ((bf16[32,24,1024]{2,1,0:T(8,128)(2,1)}), bf16[32,24,1024]{2,1,0:T(8,128)(2,1)S(1)}, u32[]{:S(2)}, u32[]{:S(2)}) async-start(bf16[32,24,1024]{2,1,0:T(8,128)(2,1)} %bitcast.16), calls=%async_computation | async-start | bytes 3145728 | tf_op jit(solution)/shard_map/all_to_all | solution.py:48
  32.1 4.7 %copy-start.27 = (s32[64,8]{0,1:T(8,128)S(1)}, s32[64,8]{0,1:T(8,128)}, u32[]{:S(2)}) copy-start(s32[64,8]{0,1:T(8,128)} %param.20) | copy-start | bytes 6148
  32.1 4.7 %copy-start.28 = (s32[64,8]{0,1:T(8,128)S(1)}, s32[64,8]{0,1:T(8,128)}, u32[]{:S(2)}) copy-start(s32[64,8]{0,1:T(8,128)} %param.18) | copy-start | bytes 6148
  32.2 4.8 %copy-start.29 = (f32[64,8]{0,1:T(8,128)S(1)}, f32[64,8]{0,1:T(8,128)}, u32[]{:S(2)}) copy-start(f32[64,8]{0,1:T(8,128)} %param.19) | copy-start | bytes 6148
  32.2 5.1 %copy-start.26 = (bf16[64,1024]{1,0:T(8,128)(2,1)S(1)}, bf16[64,1024]{1,0:T(8,128)(2,1)}, u32[]{:S(2)}) copy-start(bf16[64,1024]{1,0:T(8,128)(2,1)} %param.15) | copy-start | bytes 393220
  33.3 24.5 %all-to-all-start.1 = ((bf16[32,24,1024]{2,1,0:T(8,128)(2,1)}), bf16[32,24,1024]{2,1,0:T(8,128)(2,1)S(1)}, u32[]{:S(2)}, u32[]{:S(2)}) async-start(bf16[32,24,1024]{2,1,0:T(8,128)(2,1)} %bitcast.138), calls=%async_computation.1 | async-start | bytes 3145728 | tf_op jit(solution)/shard_map/all_to_all | solution.py:47
  36.9 2.2 %copy-start.18 = (bf16[32,24,1024]{2,1,0:T(8,128)(2,1)S(1)}, bf16[32,24,1024]{2,1,0:T(8,128)(2,1)}, u32[]{:S(2)}) copy-start(bf16[32,24,1024]{2,1,0:T(8,128)(2,1)} %copy-done.17) | copy-start | bytes 4718596
  39.3 30.0 %copy-start.7 = (bf16[8,4,24,1024]{3,2,0,1:T(8,128)(2,1)}, bf16[8,4,24,1024]{3,2,0,1:T(8,128)(2,1)S(1)}, u32[]{:S(2)}) copy-start(bf16[8,4,24,1024]{3,2,0,1:T(8,128)(2,1)S(1)} %copy.48) | copy-start | bytes 4718596
  58.9 25.2 %all-to-all-start.4 = ((bf16[32,24,1024]{2,1,0:T(8,128)(2,1)}), bf16[32,24,1024]{2,1,0:T(8,128)(2,1)}, u32[]{:S(2)}, u32[]{:S(2)}) async-start(bf16[32,24,1024]{2,1,0:T(8,128)(2,1)} %bitcast.139), calls=%async_computation.4 | async-start | bytes 3145728 | tf_op jit(solution)/shard_map/all_to_all | solution.py:47
  64.8 3.5 %copy-start.11 = (bf16[4,1024,512]{2,1,0:T(8,128)(2,1)S(1)}, bf16[4,1024,512]{2,1,0:T(8,128)(2,1)}, u32[]{:S(2)}) copy-start(bf16[4,1024,512]{2,1,0:T(8,128)(2,1)} %param.28) | copy-start | bytes 12582916
  68.2 6.5 %copy-start.4 = (bf16[4,192,512]{2,1,0:T(8,128)(2,1)}, bf16[4,192,512]{2,1,0:T(8,128)(2,1)S(1)}, u32[]{:S(2)}) copy-start(bf16[4,192,512]{2,1,0:T(8,128)(2,1)S(1)} %convolution_convert_fusion.4) | copy-start | bytes 2359300
  68.2 2.8 %copy-start.30 = (bf16[4,512,1024]{2,1,0:T(8,128)(2,1)S(1)}, bf16[4,512,1024]{2,1,0:T(8,128)(2,1)}, u32[]{:S(2)}) copy-start(bf16[4,512,1024]{2,1,0:T(8,128)(2,1)} %param.29) | copy-start | bytes 12582916
  69.3 3.6 %copy-start.13 = (bf16[4,192,512]{2,1,0:T(8,128)(2,1)}, bf16[4,192,512]{2,1,0:T(8,128)(2,1)S(1)}, u32[]{:S(2)}) copy-start(bf16[4,192,512]{2,1,0:T(8,128)(2,1)S(1)} %convolution_convert_fusion.5) | copy-start | bytes 2359300
  71.0 2.2 %copy-start.2 = (bf16[4,1024,512]{2,1,0:T(8,128)(2,1)S(1)}, bf16[4,1024,512]{2,1,0:T(8,128)(2,1)}, u32[]{:S(2)}) copy-start(bf16[4,1024,512]{2,1,0:T(8,128)(2,1)} %param.27) | copy-start | bytes 12582916
  72.8 1.9 %copy-start.19 = (bf16[4,192,512]{2,1,0:T(8,128)(2,1)}, bf16[4,192,512]{2,1,0:T(8,128)(2,1)S(1)}, u32[]{:S(2)}) copy-start(bf16[4,192,512]{2,1,0:T(8,128)(2,1)S(1)} %get-tuple-element.39) | copy-start | bytes 2359300
  72.9 1.9 %copy-start.22 = (f32[4,192,512]{2,1,0:T(8,128)}, f32[4,192,512]{2,1,0:T(8,128)S(1)}, u32[]{:S(2)}) copy-start(f32[4,192,512]{2,1,0:T(8,128)S(1)} %get-tuple-element.40) | copy-start | bytes 4718596
  84.1 25.2 %all-to-all-start.2 = ((bf16[4,192,1024]{2,0,1:T(4,128)(2,1)}), bf16[4,192,1024]{2,0,1:T(4,128)(2,1)}, u32[]{:S(2)}, u32[]{:S(2)}) async-start(bf16[4,192,1024]{2,0,1:T(4,128)(2,1)} %copy.50), calls=%async_computation.2 | async-start | bytes 3145728 | tf_op jit(solution)/shard_map/all_to_all | solution.py:50
  90.4 4.1 %copy-start.20 = (bf16[4,192,512]{2,1,0:T(8,128)(2,1)S(1)}, bf16[4,192,512]{2,1,0:T(8,128)(2,1)}, u32[]{:S(2)}) copy-start(bf16[4,192,512]{2,1,0:T(8,128)(2,1)} %copy-done.19) | copy-start | bytes 2359300
  114.5 25.2 %all-to-all-start.3 = ((bf16[32,24,1024]{2,1,0:T(8,128)(2,1)}), bf16[32,24,1024]{2,1,0:T(8,128)(2,1)}, u32[]{:S(2)}, u32[]{:S(2)}) async-start(bf16[32,24,1024]{2,1,0:T(8,128)(2,1)} %bitcast.142), calls=%async_computation.3 | async-start | bytes 3145728 | tf_op jit(solution)/shard_map/all_to_all | solution.py:48
  118.8 4.3 %copy-start.5 = (bf16[4,192,512]{2,1,0:T(8,128)(2,1)S(1)}, bf16[4,192,512]{2,1,0:T(8,128)(2,1)}, u32[]{:S(2)}) copy-start(bf16[4,192,512]{2,1,0:T(8,128)(2,1)} %copy-done.4) | copy-start | bytes 2359300
  118.8 4.2 %copy-start.8 = (bf16[8,4,24,1024]{3,2,0,1:T(8,128)(2,1)S(1)}, bf16[8,4,24,1024]{3,2,0,1:T(8,128)(2,1)}, u32[]{:S(2)}) copy-start(bf16[8,4,24,1024]{3,2,0,1:T(8,128)(2,1)} %copy-done.7) | copy-start | bytes 4718596
  118.8 4.2 %copy-start.14 = (bf16[4,192,512]{2,1,0:T(8,128)(2,1)S(1)}, bf16[4,192,512]{2,1,0:T(8,128)(2,1)}, u32[]{:S(2)}) copy-start(bf16[4,192,512]{2,1,0:T(8,128)(2,1)} %copy-done.13) | copy-start | bytes 2359300
  123.1 4.8 %copy-start.23 = (f32[4,192,512]{2,1,0:T(8,128)S(1)}, f32[4,192,512]{2,1,0:T(8,128)}, u32[]{:S(2)}) copy-start(f32[4,192,512]{2,1,0:T(8,128)} %copy-done.22) | copy-start | bytes 4718596
  139.7 1.7 copy-start.6
  139.7 1.8 %copy-start.15 = (bf16[4,192,512]{2,1,0:T(8,128)(2,1)S(1)}, bf16[4,192,512]{2,1,0:T(8,128)(2,1)}, u32[]{:S(2)}) copy-start(bf16[4,192,512]{2,1,0:T(8,128)(2,1)} %convolution_convert_fusion.3) | copy-start | bytes 2359300
  141.4 4.6 %copy-start.9 = (bf16[8,4,24,1024]{3,2,0,1:T(8,128)(2,1)}, bf16[8,4,24,1024]{3,2,0,1:T(8,128)(2,1)S(1)}, u32[]{:S(2)}) copy-start(bf16[8,4,24,1024]{3,2,0,1:T(8,128)(2,1)S(1)} %copy.53) | copy-start | bytes 4718596
  141.5 4.5 %copy-start.3 = (bf16[4,1024,512]{2,1,0:T(8,128)(2,1)S(1)}, bf16[4,1024,512]{2,1,0:T(8,128)(2,1)}, u32[]{:S(2)}) copy-start(bf16[4,1024,512]{2,1,0:T(8,128)(2,1)} %param.24) | copy-start | bytes 12582916
  146.0 3.0 %copy-start.12 = (bf16[4,1024,512]{2,1,0:T(8,128)(2,1)S(1)}, bf16[4,1024,512]{2,1,0:T(8,128)(2,1)}, u32[]{:S(2)}) copy-start(bf16[4,1024,512]{2,1,0:T(8,128)(2,1)} %param.25) | copy-start | bytes 12582916
  153.0 25.2 %all-to-all-start.5 = ((bf16[4,192,1024]{2,0,1:T(4,128)(2,1)}), bf16[4,192,1024]{2,0,1:T(4,128)(2,1)}, u32[]{:S(2)}, u32[]{:S(2)}) async-start(bf16[4,192,1024]{2,0,1:T(4,128)(2,1)} %copy.55), calls=%async_computation.5 | async-start | bytes 3145728 | tf_op jit(solution)/shard_map/all_to_all | solution.py:50
  157.5 6.0 %copy-start.10 = (bf16[8,4,24,1024]{3,2,0,1:T(8,128)(2,1)S(1)}, bf16[8,4,24,1024]{3,2,0,1:T(8,128)(2,1)}, u32[]{:S(2)}) copy-start(bf16[8,4,24,1024]{3,2,0,1:T(8,128)(2,1)} %copy-done.9) | copy-start | bytes 4718596
  163.5 4.7 %copy-start.25 = (f32[4,192,512]{2,1,0:T(8,128)S(1)}, f32[4,192,512]{2,1,0:T(8,128)}, u32[]{:S(2)}) copy-start(f32[4,192,512]{2,1,0:T(8,128)} %copy-done.24) | copy-start | bytes 4718596
  (6 other events, 7.6 us)
where the time goes:
time: 182 us; the launch traced here: 181 us
  waiting for transfers between devices  65.2 us (36%)
  matrix products  65.1 us (36%)
  starting transfers between devices  26.6 us (15%)
  local copies, waits for them, and re-layouts  21.6 us (12%)
    all_to_all x2, waiting for transfers between devices, layer_backward(): lax.all_to_all(z_send.reshape(n_experts, capacity, model_dim), 'expert',...  26.2 us
    all_to_all x2, waiting for transfers between devices, layer_backward(): lax.all_to_all(x_send.reshape(n_experts, capacity, model_dim), 'expert',...  24 us
    all_to_all x2, waiting for transfers between devices, layer_backward(): lax.all_to_all(dx_rows, 'expert', 1, 0, tiled=True)  15.1 us
    dot_general x2, matrix products, expert_grads(): jnp.einsum('erd,erf->edf', x_rows, d_gate, preferred_element_type=jnp.flo...  10.8 us
    all_to_all x2, starting transfers between devices, layer_backward(): lax.all_to_all(z_send.reshape(n_experts, capacity, model_dim), 'expert',...  9.76 us
    dot_general x2, matrix products, expert_grads(): jnp.einsum('erd,erf->edf', x_rows, d_up, preferred_element_type=jnp.float32)  9.54 us
    dot_general x2, matrix products, expert_grads(): jnp.einsum('erf,erd->efd', hidden, dz_rows, preferred_element_type=jnp.fl...  9.49 us
    all_to_all x2, starting transfers between devices, layer_backward(): lax.all_to_all(dx_rows, 'expert', 1, 0, tiled=True)  8.99 us
  transfers between devices with their start and end apart: 6, of which 6 were waited for; matrix products, arithmetic and copies ran while one was open for 32% of the time, Pallas kernels for 0%

commit v1 on v0

v1 whole, which is shorter than its diff:
```python
import functools

import jax
import jax.numpy as jnp
from jax import lax
from jax.experimental import pallas as pl
from jax.experimental.pallas import tpu as pltpu
from jax.sharding import PartitionSpec as P

GROUP = 8
EXP = 4
CAP = 24
TOK = 64
DIM = 1024
FFN = 512
PAIR = 2 * CAP
ROWS = GROUP * CAP
NK = 4
KC = DIM // NK
BF = jnp.bfloat16
F32 = jnp.float32
NT = (((1,), (1,)), ((), ()))
TN = (((0,), (0,)), ((), ()))


def dot(a, b, dims=(((1,), (0,)), ((), ()))):
    return lax.dot_general(a, b, dims, preferred_element_type=F32)


def exchange_kernel(
    y_hbm, dy_hbm, x_hbm, e2, g2, s2, e1, g1, s1, wg2, wu2, wd2, wg1, wu1, wd1,
    u2_o, z2_o, h2_o, a2_o, b2_o, u1_o, z1_o, h1_o, a1_o, b1_o, t1a_o, t1b_o, t1c_o, t1d_o, dym_o,
    wg, wu, wd, tok, dmid, route, sel, gate, u, z, actA, actB, hid, dA, dB, dh, dxk, s_oth, s_rcv, s_own, rs_rcv,
    w_sem, l_sem, r_send, r_recv, g_send, g_recv, d_send, d_recv, c_send, c_recv, p_send, p_recv, o_sem,
):
    me = lax.axis_index("expert")
    core = lax.rem(me, 2)
    bx = lax.rem(me // 2, 2)
    by = me // 4
    partner = me + 1 - 2 * core
    devs = (None, me + 2 - 4 * bx, me + 4 - 8 * by, me + 6 - 4 * bx - 8 * by)

    def remote(src, dst, ss, rs, dev):
        return pltpu.make_async_remote_copy(
            src_ref=src, dst_ref=dst, send_sem=ss, recv_sem=rs, device_id={"expert": dev}, device_id_type=pl.DeviceIdType.MESH
        )

    local = [pltpu.make_async_copy(src, tok.at[a, 0], l_sem.at[a]) for a, src in enumerate((y_hbm, dy_hbm, x_hbm))]
    for c in local:
        c.start()
    wcopies = []
    for n, (src, dst) in enumerate(((wg2, wg.at[1]), (wu2, wu.at[1]), (wd2, wd.at[1]), (wg1, wg.at[0]), (wu1, wu.at[0]), (wd1, wd.at[0]))):
        wcopies.append(pltpu.make_async_copy(src, dst, w_sem.at[n]))

    def doubled(v):
        return jnp.concatenate([v, v], axis=1)

    for lay, (e, g, s) in enumerate(((e1, g1, s1), (e2, g2, s2))):
        code = jnp.where(s[...] >= 0, e[...] * PAIR + s[...], -1000000).astype(F32)
        route[0, 2 * lay] = doubled(code)
        route[0, 2 * lay + 1] = doubled(g[...])

    barrier = pltpu.get_barrier_semaphore()
    for dev in (partner,) + devs[1:]:
        pl.semaphore_signal(barrier, inc=1, device_id={"expert": dev}, device_id_type=pl.DeviceIdType.MESH)
    pl.semaphore_wait(barrier, 4)

    def gather(view, send, recv):
        direct = [remote(view(0), view(2 * p), send.at[p], recv.at[2 * p], devs[p]) for p in (1, 2, 3)]
        own = remote(view(0), view(1), send.at[0], recv.at[1], partner)
        fwd = [remote(view(2 * p), view(2 * p + 1), send.at[3 + p], recv.at[2 * p + 1], partner) for p in (1, 2, 3)]
        return direct, own, fwd

    def launch(g):
        for c in g[0]:
            c.start()
        g[1].start()

    def forward(g):
        for c, f in zip(g[0], g[2]):
            c.wait_recv()
            f.start()

    rt = gather(lambda k: route.at[k], r_send, r_recv)
    tg = [gather(lambda k, a=a: tok.at[a, k], g_send.at[a], g_recv.at[a]) for a in range(3)]
    launch(rt)
    for a in range(3):
        local[a].wait()
        launch(tg[a])
    for c in wcopies:
        c.start()

    forward(rt)
    rt[1].wait_recv()
    for f in rt[2]:
        f.wait_recv()

    lane = lax.broadcasted_iota(jnp.int32, (8, 2 * TOK), 1)
    row = lax.broadcasted_iota(jnp.int32, (EXP * PAIR, 2 * TOK), 0).astype(F32)
    base = (me * (EXP * PAIR)).astype(F32)

    def build_select(lay):
        for p in range(4):
            code = jnp.where(lane < TOK, route[2 * p, 2 * lay], route[2 * p + 1, 2 * lay] + CAP) - base
            gates = jnp.where(lane < TOK, route[2 * p, 2 * lay + 1], route[2 * p + 1, 2 * lay + 1])
            hit = jnp.zeros((EXP * PAIR, 2 * TOK), F32)
            total = jnp.zeros((EXP * PAIR, 2 * TOK), F32)
            for j in range(8):
                match = row == code[j : j + 1, :]
                hit = jnp.where(match, 1.0, hit)
                total = jnp.where(match, gates[j : j + 1, :], total)
            sel[lay, p] = hit.astype(BF)
            gate[lay, p] = jnp.broadcast_to(jnp.sum(total, axis=1, keepdims=True), (EXP * PAIR, 128))

    build_select(1)

    def put_rows(dst, p, cols, rows):
        for e in range(EXP):
            dst[e, p * PAIR : (p + 1) * PAIR, cols] = rows[e * PAIR : (e + 1) * PAIR, :]

    def pick_rows(lay, p, block):
        return dot(sel[lay, p], block)

    def build_u(lay, a, p):
        for k in range(NK):
            cols = slice(k * KC, (k + 1) * KC)
            block = jnp.concatenate([tok[a, 2 * p, :, cols], tok[a, 2 * p + 1, :, cols]], axis=0)
            put_rows(u.at[lay], p, cols, pick_rows(lay, p, block).astype(BF))

    def build_z(lay, p, cols, first, second):
        rows = pick_rows(lay, p, jnp.concatenate([first, second], axis=0))
        g = gate[lay, p]
        rows = jnp.concatenate([rows[:, i * 128 : (i + 1) * 128] * g for i in range(KC // 128)], axis=1)
        put_rows(z.at[lay], p, cols, rows.astype(BF))

    def recompute(lay):
        def body(e, _):
            actA[lay, e] = dot(u[lay, e], wg[lay, e]).astype(BF)
            actB[lay, e] = dot(u[lay, e], wu[lay, e]).astype(BF)
            return 0

        lax.fori_loop(0, EXP, body, 0)

    def activation_grads(lay, e, d_hid):
        a = actA[lay, e].astype(F32)
        b = actB[lay, e].astype(F32)
        sig = jax.nn.sigmoid(a)
        silu = a * sig
        hid[lay, e] = (silu * b).astype(BF)
        dA[lay, e] = (d_hid * b * sig * (1.0 + a * (1.0 - sig))).astype(BF)
        dB[lay, e] = (d_hid * silu).astype(BF)

    def return_rows(lay, k):
        def body(e, _):
            cols = slice(k * KC, (k + 1) * KC)
            rows = dot(dA[lay, e], wg[lay, e, cols, :], NT) + dot(dB[lay, e], wu[lay, e, cols, :], NT)
            rows = rows.astype(BF)
            for p in range(4):
                dxk[p, e] = rows[p * PAIR : (p + 1) * PAIR, :]
            return 0

        lax.fori_loop(0, EXP, body, 0)
        for p in range(4):
            part = dot(sel[lay, p], dxk[p].reshape(EXP * PAIR, KC), TN)
            s_own[lay, k, p] = part[:TOK, :]
            s_oth[lay, k, p] = part[TOK:, :]

    chip = [
        [remote(s_oth.at[lay, k], s_rcv.at[lay, k], c_send.at[lay, k], c_recv.at[lay, k], partner) for k in range(NK)]
        for lay in range(2)
    ]
    scatter = [
        [remote(s_own.at[1, k, p], rs_rcv.at[k, p], p_send.at[k, p], p_recv.at[k, p], devs[p]) for p in (1, 2, 3)]
        for k in range(NK)
    ]

    forward(tg[0])
    tg[0][1].wait_recv()
    for f in tg[0][2]:
        f.wait_recv()
    for p in range(4):
        build_u(1, 0, p)
    wcopies[0].wait()
    wcopies[1].wait()
    recompute(1)
    forward(tg[1])
    build_select(0)
    tg[1][1].wait_recv()
    for f in tg[1][2]:
        f.wait_recv()
    for p in range(4):
        for k in range(NK):
            cols = slice(k * KC, (k + 1) * KC)
            build_z(1, p, cols, tok[1, 2 * p, :, cols], tok[1, 2 * p + 1, :, cols])
    wcopies[2].wait()

    def body2(e, _):
        activation_grads(1, e, dot(z[1, e], wd[1, e], NT))
        return 0

    lax.fori_loop(0, EXP, body2, 0)

    outs = []

    def save(n, src, dst):
        c = pltpu.make_async_copy(src, dst, o_sem.at[n])
        c.start()
        outs.append(c)

    save(0, u.at[1], u2_o)
    save(1, z.at[1], z2_o)
    save(2, hid.at[1], h2_o)
    save(3, dA.at[1], a2_o)
    save(4, dB.at[1], b2_o)

    def combine(lay, k):
        chip[lay][k].wait_recv()
        for p in range(4):
            s_own[lay, k, p] = s_own[lay, k, p] + s_rcv[lay, k, p]

    for k in range(NK):
        return_rows(1, k)
        chip[1][k].start()
        if k:
            combine(1, k - 1)
            for c in scatter[k - 1]:
                c.start()
    combine(1, NK - 1)
    for c in scatter[NK - 1]:
        c.start()

    forward(tg[2])
    tg[2][1].wait_recv()
    for f in tg[2][2]:
        f.wait_recv()
    for p in range(4):
        build_u(0, 2, p)
    save(5, u.at[0], u1_o)
    wcopies[3].wait()
    wcopies[4].wait()
    recompute(0)

    mid = [gather(lambda s, k=k: dmid.at[k, s], d_send.at[k], d_recv.at[k]) for k in range(NK)]
    for k in range(NK):
        for c in scatter[k]:
            c.wait_recv()
        total = s_own[1, k, 0] + rs_rcv[k, 1] + rs_rcv[k, 2] + rs_rcv[k, 3]
        dmid[k, 0] = (tok[1, 0, :, k * KC : (k + 1) * KC].astype(F32) + total).astype(BF)
        launch(mid[k])
    wcopies[5].wait()

    def middle(k):
        mid[k][1].wait_recv()
        for f in mid[k][2]:
            f.wait_recv()
        cols = slice(k * KC, (k + 1) * KC)
        for p in range(4):
            build_z(0, p, cols, dmid[k, 2 * p], dmid[k, 2 * p + 1])

        def body(e, _):
            part = dot(z[0, e, :, cols], wd[0, e, :, cols], NT)
            dh[e] = part if k == 0 else dh[e] + part
            return 0

        lax.fori_loop(0, EXP, body, 0)

    for k in range(NK):
        forward(mid[k])
        if k:
            middle(k - 1)
    for k in range(NK):
        dym_c = pltpu.make_async_copy(dmid.at[k, 0], dym_o.at[:, pl.ds(k * KC, KC)], o_sem.at[12 + k])
        dym_c.start()
        outs.append(dym_c)
    middle(NK - 1)
    save(6, z.at[0], z1_o)

    def body1(e, _):
        activation_grads(0, e, dh[e])
        return 0

    lax.fori_loop(0, EXP, body1, 0)
    save(7, hid.at[0], h1_o)
    save(8, dA.at[0], a1_o)
    save(9, dB.at[0], b1_o)

    def finish(k):
        combine(0, k)
        for p, t1_o in enumerate((t1a_o, t1b_o, t1c_o, t1d_o)):
            c = pltpu.make_async_copy(s_own.at[0, k, p], t1_o.at[:, pl.ds(k * KC, KC)], o_sem.at[16 + 4 * k + p])
            c.start()
            outs.append(c)

    for k in range(NK):
        return_rows(0, k)
        chip[0][k].start()
        if k:
            finish(k - 1)
    finish(NK - 1)

    for g in [rt] + tg + mid:
        for c in g[0] + [g[1]] + g[2]:
            c.wait_send()
    for lay in range(2):
        for c in chip[lay]:
            c.wait_send()
    for cs in scatter:
        for c in cs:
            c.wait_send()
    for c in outs:
        c.wait()


def exchange(*args):
    rows = lambda n: jax.ShapeDtypeStruct((EXP, ROWS, n), BF)
    per_layer = [rows(DIM), rows(DIM), rows(FFN), rows(FFN), rows(FFN)]
    any_spec = pl.BlockSpec(memory_space=pl.ANY)
    vmem_spec = pl.BlockSpec(memory_space=pltpu.VMEM)
    dma = pltpu.SemaphoreType.DMA
    return pl.pallas_call(
        exchange_kernel,
        out_shape=per_layer + per_layer + [jax.ShapeDtypeStruct((TOK, DIM), F32)] * 4 + [jax.ShapeDtypeStruct((TOK, DIM), BF)],
        in_specs=[any_spec] * 3 + [vmem_spec] * 6 + [any_spec] * 6,
        out_specs=[any_spec] * 15,
        scratch_shapes=[
            pltpu.VMEM((2, EXP, DIM, FFN), BF),
            pltpu.VMEM((2, EXP, DIM, FFN), BF),
            pltpu.VMEM((2, EXP, FFN, DIM), BF),
            pltpu.VMEM((3, GROUP, TOK, DIM), BF),
            pltpu.VMEM((NK, GROUP, TOK, KC), BF),
            pltpu.VMEM((GROUP, 4, 8, 2 * TOK), F32),
            pltpu.VMEM((2, 4, EXP * PAIR, 2 * TOK), BF),
            pltpu.VMEM((2, 4, EXP * PAIR, 128), F32),
            pltpu.VMEM((2, EXP, ROWS, DIM), BF),
            pltpu.VMEM((2, EXP, ROWS, DIM), BF),
            pltpu.VMEM((2, EXP, ROWS, FFN), BF),
            pltpu.VMEM((2, EXP, ROWS, FFN), BF),
            pltpu.VMEM((2, EXP, ROWS, FFN), BF),
            pltpu.VMEM((2, EXP, ROWS, FFN), BF),
            pltpu.VMEM((2, EXP, ROWS, FFN), BF),
            pltpu.VMEM((EXP, ROWS, FFN), F32),
            pltpu.VMEM((4, EXP, PAIR, KC), BF),
            pltpu.VMEM((2, NK, 4, TOK, KC), F32),
            pltpu.VMEM((2, NK, 4, TOK, KC), F32),
            pltpu.VMEM((2, NK, 4, TOK, KC), F32),
            pltpu.VMEM((NK, 4, TOK, KC), F32),
            dma((6,)),
            dma((3,)),
            dma((7,)),
            dma((8,)),
            dma((3, 7)),
            dma((3, 8)),
            dma((NK, 7)),
            dma((NK, 8)),
            dma((2, NK)),
            dma((2, NK)),
            dma((NK, 4)),
            dma((NK, 4)),
            dma((32,)),
        ],
        compiler_params=pltpu.CompilerParams(collective_id=0, has_side_effects=True, vmem_limit_bytes=60 * 2**20),
        cost_estimate=pl.CostEstimate(flops=10**10, bytes_accessed=40 * 2**20, transcendentals=0),
    )(*args)


def weight_grad_kernel(u2, z2, h2, a2, b2, u1, z1, h1, a1, b1, g2, p2, d2, g1, p1, d1):
    step = pl.program_id(0)

    def layer(u, z, h, a, b, g_o, p_o, d_o):
        g_o[0] = dot(u[0], a[0], TN)
        p_o[0] = dot(u[0], b[0], TN)
        d_o[0] = dot(h[0], z[0], TN)

    @pl.when(step < 8)
    def _():
        layer(u2, z2, h2, a2, b2, g2, p2, d2)

    @pl.when(step >= 8)
    def _():
        layer(u1, z1, h1, a1, b1, g1, p1, d1)


def weight_grads(*rows):
    def at(lay, split):
        def index(s):
            t = jnp.clip(s - 8 * lay, 0, 7)
            return (t // 2,) + ((0, t % 2) if split == "cols" else (t % 2, 0) if split == "rows" else (0, 0))

        return index

    half_d, half_f = DIM // 2, FFN // 2
    ins, outs, shapes = [], [], []
    for lay in range(2):
        ins += [
            pl.BlockSpec((1, ROWS, half_d), at(lay, "cols")),
            pl.BlockSpec((1, ROWS, DIM), at(lay, "")),
            pl.BlockSpec((1, ROWS, half_f), at(lay, "cols")),
            pl.BlockSpec((1, ROWS, FFN), at(lay, "")),
            pl.BlockSpec((1, ROWS, FFN), at(lay, "")),
        ]
        outs += [pl.BlockSpec((1, half_d, FFN), at(lay, "rows"))] * 2 + [pl.BlockSpec((1, half_f, DIM), at(lay, "rows"))]
        up = jax.ShapeDtypeStruct((EXP, DIM, FFN), F32)
        shapes += [up, up, jax.ShapeDtypeStruct((EXP, FFN, DIM), F32)]
    return pl.pallas_call(
        weight_grad_kernel,
        grid=(16,),
        in_specs=ins,
        out_specs=outs,
        out_shape=shapes,
        compiler_params=pltpu.CompilerParams(vmem_limit_bytes=60 * 2**20),
        cost_estimate=pl.CostEstimate(flops=6 * 10**9, bytes_accessed=62 * 2**20, transcendentals=0),
    )(*rows)


def solution(mesh):
    tok_spec = P(("data", "expert"), None)
    weight_spec = P("expert", None, None)
    grad_spec = P(("data", "expert"), None, None)

    def local_step(x_tokens, y_mid, dy_out, experts_one, gates_one, slots_one, experts_two, gates_two, slots_two, w_gate_one, w_up_one, w_down_one, w_gate_two, w_up_two, w_down_two):
        res = exchange(
            y_mid, dy_out, x_tokens, experts_two.T, gates_two.T, slots_two.T, experts_one.T, gates_one.T, slots_one.T,
            w_gate_two, w_up_two, w_down_two, w_gate_one, w_up_one, w_down_one,
        )
        part, mid = res[10:14], res[14]
        back = [lax.ppermute(part[p], "expert", [(i, i ^ (2 * p)) for i in range(GROUP)]) for p in (1, 2, 3)]
        grads = weight_grads(*res[:10])
        total = part[0] + back[0] + back[1] + back[2]
        dx = (mid.astype(F32) + total).astype(BF)
        return (dx, grads[3], grads[4], grads[5], grads[0], grads[1], grads[2])

    return jax.shard_map(local_step, mesh=mesh, in_specs=(tok_spec,) * 9 + (weight_spec,) * 6, out_specs=(tok_spec,) + (grad_spec,) * 6, check_vma=False)
```

time: 182 us -> 90.7 us (0.50)
  Pallas kernels: 0 us -> 85.1 us
  waiting for transfers between devices: 65.2 us -> 0.01 us
  matrix products: 65.1 us -> 0 us
  starting transfers between devices: 26.6 us -> 3.52 us
  local copies, waits for them, and re-layouts: 21.6 us -> 0.01 us
    pallas_call x0 -> x2, Pallas kernels: none -> 85.1 us  [the longest x1 60.2 us: exchange(): pl.pallas_call(exchange_kernel, out_shape=per_layer + per_layer + [jax.Sh...]
    all_to_all x6 -> x0, waiting for transfers between devices: 65.2 us -> none  [the longest x2 26.2 us: layer_backward(): lax.all_to_all(z_send.reshape(n_experts, capacity, model_dim), 'expert',...]
    dot_general x22 -> x0, matrix products: 65.1 us -> none  [the longest x2 10.8 us: expert_grads(): jnp.einsum('erd,erf->edf', x_rows, d_gate, preferred_element_type=jnp.flo...]
    all_to_all x6 -> x0, starting transfers between devices: 26.6 us -> none  [the longest x2 9.76 us: layer_backward(): lax.all_to_all(z_send.reshape(n_experts, capacity, model_dim), 'expert',...]
    all_to_all x8 -> x0, local copies, waits for them, and re-layouts: 8.98 us -> none  [the longest x4 4.05 us: layer_backward(): lax.all_to_all(dx_rows, 'expert', 1, 0, tiled=True)]
    unnamed x64 -> x4, local copies, waits for them, and re-layouts: 6.91 us -> 0.01 us
    convert_element_type x2 -> x0, local copies, waits for them, and re-layouts: 4.73 us -> none  [expert_grads(): (jnp.einsum('erf,edf->erd', d_gate, w_gate, preferred_element_type=jnp.fl...]
    ppermute x0 -> x3, starting transfers between devices: none -> 3.52 us  [local_step(): lax.ppermute(part[p], 'expert', [(i, i ^ 2 * p) for i in range(GROUP)])]
  transfers between devices with their start and end apart: 6 -> 3, of which waited for: 6 -> 0; matrix products, arithmetic and copies ran while one was open for 32% -> 0% of each run, Pallas kernels for 0% -> 28%
where the time goes in v1:
time: 90.7 us; the launch traced here: 90.1 us
  Pallas kernels  85.1 us (94%)
  starting transfers between devices  3.52 us (4%)
    pallas_call x1, Pallas kernels, exchange(): pl.pallas_call(exchange_kernel, out_shape=per_layer + per_layer + [jax.Sh...  60.2 us
    pallas_call x1, Pallas kernels, weight_grads(): pl.pallas_call(weight_grad_kernel, grid=(16,), in_specs=ins, out_specs=ou...  25 us
    ppermute x3, starting transfers between devices, local_step(): lax.ppermute(part[p], 'expert', [(i, i ^ 2 * p) for i in range(GROUP)])  3.52 us
  transfers between devices with their start and end apart: 3, of which 0 were waited for; matrix products, arithmetic and copies ran while one was open for 0% of the time, Pallas kernels for 28%

profile of v1, /device:TPU:0, one launch (start us, length us, event | category | flops | bytes accessed | tf_op | source)
XLA Modules:
  0.0 90.1 jit_solution(10764365058517149252)
XLA Ops:
  0.6 60.2 %shard_map.198 = (bf16[4,192,1024]{2,1,0:T(8,128)(2,1)}, bf16[4,192,1024]{2,1,0:T(8,128)(2,1)}, bf16[4,192,512]{2,1,0:T(8,128)(2,1)}, bf16[4,192,512]{2,1,0:T(8,...) custom-call(bf16[64,1024]{1,0:T(8,128)(2,1)} %y_hbm.1, ...), custom_call_target="tpu_custom_call" | custom-call | flops 10000000000 | bytes 41943040 | tf_op jit(solution)/shard_map/pallas_call | solution.py:320
  60.8 0.6 collective-permute-start
  61.4 0.5 collective-permute-start.1
  62.0 2.4 %collective-permute-start.2 = (f32[64,1024]{1,0:T(8,128)}, f32[64,1024]{1,0:T(8,128)S(1)}, u32[]{:S(2)}, u32[]{:S(2)}) collective-permute-start(f32[64,1024]{1,0:T(8,128)} %get-tuple-element.32), channel_id=1, source_target_pairs={{0,6},{1,7},{2,4},{3,5},{4,2},{5,3},{6,0},{7,1},{8,14},{9,15},{10,... | collective-permute-start | bytes 786440 | tf_op jit(solution)/shard_map/ppermute | solution.py:426
  64.3 0.0 copy-start
  64.3 0.0 copy-start.1
  64.3 25.0 %shard_map.199 = (f32[4,1024,512]{2,1,0:T(8,128)}, f32[4,1024,512]{2,1,0:T(8,128)}, f32[4,512,1024]{2,1,0:T(8,128)}, f32[4,1024,512]{2,1,0:T(8,128)}, f32[4,1024,512]{2,1,0:T(8,128)}, /*index=5*/f32[4,512,1024]{2,1,0:T(8,128)}) custom-call(bf16[4,192,1024]{2,1,0:T(8,128)(2,1)} %get-tuple-element.33.u2, bf16[4,192,1024]{2,1,0:T(8,128)(2,1)} %get-tuple-element.34.z2, ...), custom_call_target="tpu_custom_call" | custom-call | flops 6000000000 | bytes 65011712 | tf_op jit(solution)/shard_map/pallas_call | solution.py:404
  89.3 0.0 collective-permute-done
  89.3 0.0 collective-permute-done.1
  89.3 0.0 collective-permute-done.2
  89.4 0.0 copy-done
  89.4 0.0 copy-done.1
  89.4 0.7 add_convert_fusion
Async XLA Ops:
  60.8 28.5 %collective-permute-start = (f32[64,1024]{1,0:T(8,128)}, f32[64,1024]{1,0:T(8,128)S(1)}, u32[]{:S(2)}, u32[]{:S(2)}) collective-permute-start(f32[64,1024]{1,0:T(8,128)} %get-tuple-element.30), channel_id=1, source_target_pairs={{0,2},{1,3},{2,0},{3,1},{4,6},{5,7},{6,4},{7,5},{8,10},{9,11},{10,... | collective-permute-start | bytes 786440 | tf_op jit(solution)/shard_map/ppermute | solution.py:426
  61.4 27.9 %collective-permute-start.1 = (f32[64,1024]{1,0:T(8,128)}, f32[64,1024]{1,0:T(8,128)S(1)}, u32[]{:S(2)}, u32[]{:S(2)}) collective-permute-start(f32[64,1024]{1,0:T(8,128)} %get-tuple-element.31), channel_id=1, source_target_pairs={{0,4},{1,5},{2,6},{3,7},{4,0},{5,1},{6,2},{7,3},{8,12},{9,13},{10,... | collective-permute-start | bytes 786440 | tf_op jit(solution)/shard_map/ppermute | solution.py:426
  62.0 27.4 %collective-permute-start.2 = (f32[64,1024]{1,0:T(8,128)}, f32[64,1024]{1,0:T(8,128)S(1)}, u32[]{:S(2)}, u32[]{:S(2)}) collective-permute-start(f32[64,1024]{1,0:T(8,128)} %get-tuple-element.32), channel_id=1, source_target_pairs={{0,6},{1,7},{2,4},{3,5},{4,2},{5,3},{6,0},{7,1},{8,14},{9,15},{10,... | collective-permute-start | bytes 786440 | tf_op jit(solution)/shard_map/ppermute | solution.py:426
  64.3 25.0 %copy-start = (f32[64,1024]{1,0:T(8,128)S(1)}, f32[64,1024]{1,0:T(8,128)}, u32[]{:S(2)}) copy-start(f32[64,1024]{1,0:T(8,128)} %get-tuple-element.29) | copy-start | bytes 786436
  64.3 25.0 %copy-start.1 = (bf16[64,1024]{1,0:T(8,128)(2,1)S(1)}, bf16[64,1024]{1,0:T(8,128)(2,1)}, u32[]{:S(2)}) copy-start(bf16[64,1024]{1,0:T(8,128)(2,1)} %get-tuple-element.28) | copy-start | bytes 393220

commit v2 on v0

v2 whole, which is shorter than its diff:
```python
import functools

import jax
import jax.numpy as jnp
from jax import lax
from jax.experimental import pallas as pl
from jax.experimental.pallas import tpu as pltpu
from jax.sharding import PartitionSpec as P

GROUP = 8
EXP = 4
CAP = 24
TOK = 64
DIM = 1024
FFN = 512
PAIR = 2 * CAP
ROWS = GROUP * CAP
NK = 4
KC = DIM // NK
BF = jnp.bfloat16
F32 = jnp.float32
NT = (((1,), (1,)), ((), ()))
TN = (((0,), (0,)), ((), ()))


def dot(a, b, dims=(((1,), (0,)), ((), ()))):
    return lax.dot_general(a, b, dims, preferred_element_type=F32)


class Copy:
    def __init__(self, copy, log):
        self.copy, self.log, self.arrived = copy, log, False

    def start(self):
        self.copy.start()
        self.log.append(self)

    def wait_recv(self):
        self.copy.wait_recv()
        self.arrived = True

    def drain(self):
        if not self.arrived:
            self.copy.wait_recv()
        self.copy.wait_send()


def exchange_kernel(
    y_hbm, dy_hbm, x_hbm, e2, g2, s2, e1, g1, s1, wg2, wu2, wd2, wg1, wu1, wd1,
    u2, z2, hid2, dab2, u1, z1, hid1, dab1, t1a, t1b, t1c, t1d, dym,
    wcat, wd, tok, dmid, raw_int, raw_gate, route, sel, selt, gate, act, dh, dx, s_oth, s_rcv, s_own, rs_rcv,
    w_sem, l_sem, r_send, r_recv, g_send, g_recv, d_send, d_recv, c_send, c_recv, p_send, p_recv,
):
    me = lax.axis_index("expert")
    core = lax.rem(me, 2)
    bx = lax.rem(me // 2, 2)
    by = me // 4
    partner = me + 1 - 2 * core
    devs = (None, me + 2 - 4 * bx, me + 4 - 8 * by, me + 6 - 4 * bx - 8 * by)
    u, z, hid, dab, t1 = (u1, u2), (z1, z2), (hid1, hid2), (dab1, dab2), (t1a, t1b, t1c, t1d)
    sent = []

    def remote(src, dst, ss, rs, dev):
        copy = pltpu.make_async_remote_copy(
            src_ref=src, dst_ref=dst, send_sem=ss, recv_sem=rs, device_id={"expert": dev}, device_id_type=pl.DeviceIdType.MESH
        )
        return Copy(copy, sent)

    local = [pltpu.make_async_copy(src, tok.at[a, 0], l_sem.at[a]) for a, src in enumerate((y_hbm, dy_hbm, x_hbm))]
    tables = ((e1, raw_int.at[0]), (s1, raw_int.at[1]), (g1, raw_gate.at[0]), (e2, raw_int.at[2]), (s2, raw_int.at[3]), (g2, raw_gate.at[1]))
    tables = [pltpu.make_async_copy(src, dst, l_sem.at[3 + n]) for n, (src, dst) in enumerate(tables)]
    for c in tables + local:
        c.start()
    left, right = pl.ds(0, FFN), pl.ds(FFN, FFN)
    weights = []
    for n, (src, dst) in enumerate(
        (
            (wg2, wcat.at[1, :, :, left]), (wu2, wcat.at[1, :, :, right]), (wd2, wd.at[1]),
            (wg1, wcat.at[0, :, :, left]), (wu1, wcat.at[0, :, :, right]), (wd1, wd.at[0]),
        )
    ):
        weights.append(pltpu.make_async_copy(src, dst, w_sem.at[n]))

    barrier = pltpu.get_barrier_semaphore()
    for dev in (partner,) + devs[1:]:
        pl.semaphore_signal(barrier, inc=1, device_id={"expert": dev}, device_id_type=pl.DeviceIdType.MESH)

    def doubled(v):
        return jnp.concatenate([v, v], axis=1)

    for c in tables:
        c.wait()
    for lay in range(2):
        experts, slots = raw_int[2 * lay], raw_int[2 * lay + 1]
        code = jnp.where(slots >= 0, experts * PAIR + slots, -1000000).astype(F32)
        route[0, 2 * lay] = doubled(code)
        route[0, 2 * lay + 1] = doubled(raw_gate[lay])

    pl.semaphore_wait(barrier, 4)

    class Gather:
        def __init__(self, view, send, recv):
            self.direct = {p: remote(view(0), view(2 * p), send.at[p], recv.at[2 * p], devs[p]) for p in (3, 1, 2)}
            self.own = remote(view(0), view(1), send.at[0], recv.at[1], partner)
            self.passed = {p: remote(view(2 * p), view(2 * p + 1), send.at[3 + p], recv.at[2 * p + 1], partner) for p in (3, 1, 2)}

        def launch(self):
            for c in self.direct.values():
                c.start()
            self.own.start()

        def forward(self):
            for p in (1, 2, 3):
                self.direct[p].wait_recv()
                self.passed[p].start()

        def rest(self):
            self.own.wait_recv()
            for p in (1, 2, 3):
                self.passed[p].wait_recv()

    routing = Gather(lambda k: route.at[k], r_send, r_recv)
    tokens = [Gather(lambda k, a=a: tok.at[a, k], g_send.at[a], g_recv.at[a]) for a in range(3)]
    routing.launch()
    for a in range(3):
        local[a].wait()
        tokens[a].launch()
    for c in weights:
        c.start()
    routing.forward()
    routing.rest()

    lane = lax.broadcasted_iota(jnp.int32, (8, 2 * TOK), 1)
    row = lax.broadcasted_iota(jnp.int32, (EXP * PAIR, 2 * TOK), 0).astype(F32)
    base = (me * (EXP * PAIR)).astype(F32)

    def build_select(lay):
        for p in range(4):
            code = jnp.where(lane < TOK, route[2 * p, 2 * lay], route[2 * p + 1, 2 * lay] + CAP) - base
            gates = jnp.where(lane < TOK, route[2 * p, 2 * lay + 1], route[2 * p + 1, 2 * lay + 1])
            hit = jnp.zeros((EXP * PAIR, 2 * TOK), F32)
            total = jnp.zeros((EXP * PAIR, 2 * TOK), F32)
            for j in range(8):
                match = row == code[j : j + 1, :]
                hit = jnp.where(match, 1.0, hit)
                total = jnp.where(match, gates[j : j + 1, :], total)
            sel[lay, p] = hit.astype(BF)
            selt[lay, p] = hit.T.astype(BF)
            gate[lay, p] = jnp.broadcast_to(jnp.sum(total, axis=1, keepdims=True), (EXP * PAIR, 128))

    build_select(1)
    build_select(0)

    def put_rows(dst, p, cols, rows):
        for e in range(EXP):
            dst[e, p * PAIR : (p + 1) * PAIR, cols] = rows[e * PAIR : (e + 1) * PAIR, :]

    def columns(k):
        return slice(k * KC, (k + 1) * KC)

    def build_u(lay, a, p):
        for k in range(NK):
            block = jnp.concatenate([tok[a, 2 * p, :, columns(k)], tok[a, 2 * p + 1, :, columns(k)]], axis=0)
            put_rows(u[lay], p, columns(k), dot(sel[lay, p], block).astype(BF))

    def build_z(lay, p, k, first, second):
        rows = dot(sel[lay, p], jnp.concatenate([first, second], axis=0))
        g = gate[lay, p]
        rows = jnp.concatenate([rows[:, i * 128 : (i + 1) * 128] * g for i in range(KC // 128)], axis=1)
        put_rows(z[lay], p, columns(k), rows.astype(BF))

    def recompute(lay):
        for e in range(EXP):
            act[e] = dot(u[lay][e], wcat[lay, e]).astype(BF)

    def expert_rows(lay, e, d_hid):
        a = act[e, :, :FFN].astype(F32)
        b = act[e, :, FFN:].astype(F32)
        sig = jax.nn.sigmoid(a)
        silu = a * sig
        hid[lay][e] = (silu * b).astype(BF)
        dab[lay][e, :, :FFN] = (d_hid * b * sig * (1.0 + a * (1.0 - sig))).astype(BF)
        dab[lay][e, :, FFN:] = (d_hid * silu).astype(BF)
        rows = dot(dab[lay][e], wcat[lay, e], NT).astype(BF)
        for p in range(4):
            dx[p, e] = rows[p * PAIR : (p + 1) * PAIR, :]

    def chip_partial(lay, k):
        for p in range(4):
            part = dot(selt[lay, p], dx[p, :, :, columns(k)].reshape(EXP * PAIR, KC))
            s_own[lay, k, p] = part[:TOK, :]
            s_oth[lay, k, p] = part[TOK:, :]

    chip = [
        [remote(s_oth.at[lay, k], s_rcv.at[lay, k], c_send.at[lay, k], c_recv.at[lay, k], partner) for k in range(NK)]
        for lay in range(2)
    ]
    scatter = [
        [remote(s_own.at[1, k, p], rs_rcv.at[k, p], p_send.at[k, p], p_recv.at[k, p], devs[p]) for p in (3, 1, 2)]
        for k in range(NK)
    ]

    tokens[0].forward()
    tokens[0].rest()
    for p in range(4):
        build_u(1, 0, p)
    weights[0].wait()
    weights[1].wait()
    recompute(1)
    tokens[1].forward()
    tokens[1].rest()
    for p in range(4):
        for k in range(NK):
            build_z(1, p, k, tok[1, 2 * p, :, columns(k)], tok[1, 2 * p + 1, :, columns(k)])
    weights[2].wait()
    for e in range(EXP):
        expert_rows(1, e, dot(z[1][e], wd[1, e], NT))
    for k in range(NK):
        chip_partial(1, k)
        chip[1][k].start()
    for k in range(NK):
        chip[1][k].wait_recv()
        for p in (3, 1, 2, 0):
            s_own[1, k, p] = s_own[1, k, p] + s_rcv[1, k, p]
        for c in scatter[k]:
            c.start()

    tokens[2].forward()
    tokens[2].rest()
    for p in range(4):
        build_u(0, 2, p)
    weights[3].wait()
    weights[4].wait()
    recompute(0)

    middle = [Gather(lambda s, k=k: dmid.at[k, s], d_send.at[k], d_recv.at[k]) for k in range(NK)]
    for k in range(NK):
        for c in scatter[k]:
            c.wait_recv()
        total = s_own[1, k, 0] + rs_rcv[k, 1] + rs_rcv[k, 2] + rs_rcv[k, 3]
        new = (tok[1, 0, :, columns(k)].astype(F32) + total).astype(BF)
        dmid[k, 0] = new
        dym[:, columns(k)] = new
        middle[k].launch()
    weights[5].wait()

    def hidden_grad(k):
        middle[k].rest()
        for p in range(4):
            build_z(0, p, k, dmid[k, 2 * p], dmid[k, 2 * p + 1])
        for e in range(EXP):
            part = dot(z[0][e, :, columns(k)], wd[0, e, :, columns(k)], NT)
            dh[e] = part if k == 0 else dh[e] + part

    for k in range(NK):
        middle[k].forward()
        if k:
            hidden_grad(k - 1)
    hidden_grad(NK - 1)
    for e in range(EXP):
        expert_rows(0, e, dh[e])
    for k in range(NK):
        chip_partial(0, k)
        chip[0][k].start()
    for k in range(NK):
        chip[0][k].wait_recv()
        for p in range(4):
            t1[p][:, columns(k)] = s_own[0, k, p] + s_rcv[0, k, p]
    for c in sent:
        c.drain()


def exchange(*args):
    rows = lambda n: pltpu.VMEM((EXP, ROWS, n), BF)
    per_layer = [rows(DIM), rows(DIM), rows(FFN), rows(2 * FFN)]
    hbm_spec = pl.BlockSpec(memory_space=pltpu.HBM)
    vmem_spec = pl.BlockSpec(memory_space=pltpu.VMEM)
    dma = pltpu.SemaphoreType.DMA
    return pl.pallas_call(
        exchange_kernel,
        out_shape=per_layer + per_layer + [pltpu.VMEM((TOK, DIM), F32)] * 4 + [pltpu.VMEM((TOK, DIM), BF)],
        in_specs=[hbm_spec] * 15,
        out_specs=[vmem_spec] * 13,
        scratch_shapes=[
            pltpu.VMEM((2, EXP, DIM, 2 * FFN), BF),
            pltpu.VMEM((2, EXP, FFN, DIM), BF),
            pltpu.VMEM((3, GROUP, TOK, DIM), BF),
            pltpu.VMEM((NK, GROUP, TOK, KC), BF),
            pltpu.VMEM((4, 8, TOK), jnp.int32),
            pltpu.VMEM((2, 8, TOK), F32),
            pltpu.VMEM((GROUP, 4, 8, 2 * TOK), F32),
            pltpu.VMEM((2, 4, EXP * PAIR, 2 * TOK), BF),
            pltpu.VMEM((2, 4, 2 * TOK, EXP * PAIR), BF),
            pltpu.VMEM((2, 4, EXP * PAIR, 128), F32),
            pltpu.VMEM((EXP, ROWS, 2 * FFN), BF),
            pltpu.VMEM((EXP, ROWS, FFN), F32),
            pltpu.VMEM((4, EXP, PAIR, DIM), BF),
            pltpu.VMEM((2, NK, 4, TOK, KC), F32),
            pltpu.VMEM((2, NK, 4, TOK, KC), F32),
            pltpu.VMEM((2, NK, 4, TOK, KC), F32),
            pltpu.VMEM((NK, 4, TOK, KC), F32),
            dma((6,)),
            dma((9,)),
            dma((7,)),
            dma((8,)),
            dma((3, 7)),
            dma((3, 8)),
            dma((NK, 7)),
            dma((NK, 8)),
            dma((2, NK)),
            dma((2, NK)),
            dma((NK, 4)),
            dma((NK, 4)),
        ],
        compiler_params=pltpu.CompilerParams(collective_id=0, has_side_effects=True, vmem_limit_bytes=K1_VMEM * 2**20),
        cost_estimate=pl.CostEstimate(flops=10**10, bytes_accessed=40 * 2**20, transcendentals=0),
    )(*[pltpu.with_memory_space_constraint(a, pltpu.HBM) for a in args])


K1_VMEM = 46
MB = 256
SLOTS = 5


def weight_grad_kernel(u2, z2, h2, ab2, u1, z1, h1, ab1, g2, p2, d2, g1, p1, d1, g_buf, p_buf, d_buf, sem):
    flying = {}
    step = 0
    for u, z, h, ab, g_o, p_o, d_o in ((u2, z2, h2, ab2, g2, p2, d2), (u1, z1, h1, ab1, g1, p1, d1)):
        for e in range(EXP):
            slot = step % SLOTS
            for c in flying.pop(step - SLOTS, []):
                c.wait()
            mine = flying.setdefault(step, [])

            def write(buf, out, m, n):
                part = pl.ds(m * MB, MB)
                c = pltpu.make_async_copy(buf.at[slot, part], out.at[e, part], sem.at[slot, n])
                c.start()
                mine.append(c)

            for m in range(DIM // MB):
                span = slice(m * MB, (m + 1) * MB)
                both = dot(u[e, :, span], ab[e], TN)
                g_buf[slot, span, :] = both[:, :FFN]
                p_buf[slot, span, :] = both[:, FFN:]
                write(g_buf, g_o, m, m)
                write(p_buf, p_o, m, DIM // MB + m)
            for m in range(FFN // MB):
                span = slice(m * MB, (m + 1) * MB)
                d_buf[slot, span, :] = dot(h[e, :, span], z[e], TN)
                write(d_buf, d_o, m, 2 * (DIM // MB) + m)
            step += 1
    for cs in flying.values():
        for c in cs:
            c.wait()


def weight_grads(*rows):
    up = jax.ShapeDtypeStruct((EXP, DIM, FFN), F32)
    shapes = [up, up, jax.ShapeDtypeStruct((EXP, FFN, DIM), F32)] * 2
    return pl.pallas_call(
        weight_grad_kernel,
        in_specs=[pl.BlockSpec(memory_space=pltpu.VMEM)] * 8,
        out_specs=[pl.BlockSpec(memory_space=pl.ANY)] * 6,
        out_shape=shapes,
        scratch_shapes=[
            pltpu.VMEM((SLOTS, DIM, FFN), F32),
            pltpu.VMEM((SLOTS, DIM, FFN), F32),
            pltpu.VMEM((SLOTS, FFN, DIM), F32),
            pltpu.SemaphoreType.DMA((SLOTS, 2 * (DIM // MB) + FFN // MB)),
        ],
        compiler_params=pltpu.CompilerParams(vmem_limit_bytes=K2_VMEM * 2**20),
        cost_estimate=pl.CostEstimate(flops=6 * 10**9, bytes_accessed=62 * 2**20, transcendentals=0),
    )(*[pltpu.with_memory_space_constraint(r, pltpu.VMEM) for r in rows])


K2_VMEM = 36


def solution(mesh):
    tok_spec = P(("data", "expert"), None)
    weight_spec = P("expert", None, None)
    grad_spec = P(("data", "expert"), None, None)

    def local_step(x_tokens, y_mid, dy_out, experts_one, gates_one, slots_one, experts_two, gates_two, slots_two, w_gate_one, w_up_one, w_down_one, w_gate_two, w_up_two, w_down_two):
        res = exchange(
            y_mid, dy_out, x_tokens, experts_two.T, gates_two.T, slots_two.T, experts_one.T, gates_one.T, slots_one.T,
            w_gate_two, w_up_two, w_down_two, w_gate_one, w_up_one, w_down_one,
        )
        part, mid = res[8:12], res[12]
        back = [lax.ppermute(part[p], "expert", [(i, i ^ (2 * p)) for i in range(GROUP)]) for p in (1, 2, 3)]
        grads = weight_grads(*res[:8])
        total = part[0] + back[0] + back[1] + back[2]
        dx = (mid.astype(F32) + total).astype(BF)
        return (dx, grads[3], grads[4], grads[5], grads[0], grads[1], grads[2])

    return jax.shard_map(local_step, mesh=mesh, in_specs=(tok_spec,) * 9 + (weight_spec,) * 6, out_specs=(tok_spec,) + (grad_spec,) * 6, check_vma=False)
```

time: 182 us -> 77 us (0.42)
  Pallas kernels: 0 us -> 71.9 us
  waiting for transfers between devices: 65.2 us -> 0.01 us
  matrix products: 65.1 us -> 0 us
  starting transfers between devices: 26.6 us -> 3.52 us
  local copies, waits for them, and re-layouts: 21.6 us -> 0 us
    pallas_call x0 -> x2, Pallas kernels: none -> 71.9 us  [the longest x1 55.4 us: exchange(): pl.pallas_call(exchange_kernel, out_shape=per_layer + per_layer + [pltpu....]
    all_to_all x6 -> x0, waiting for transfers between devices: 65.2 us -> none  [the longest x2 26.2 us: layer_backward(): lax.all_to_all(z_send.reshape(n_experts, capacity, model_dim), 'expert',...]
    dot_general x22 -> x0, matrix products: 65.1 us -> none  [the longest x2 10.8 us: expert_grads(): jnp.einsum('erd,erf->edf', x_rows, d_gate, preferred_element_type=jnp.flo...]
    all_to_all x6 -> x0, starting transfers between devices: 26.6 us -> none  [the longest x2 9.76 us: layer_backward(): lax.all_to_all(z_send.reshape(n_experts, capacity, model_dim), 'expert',...]
    all_to_all x8 -> x0, local copies, waits for them, and re-layouts: 8.98 us -> none  [the longest x4 4.05 us: layer_backward(): lax.all_to_all(dx_rows, 'expert', 1, 0, tiled=True)]
    unnamed x64 -> x0, local copies, waits for them, and re-layouts: 6.91 us -> none
    convert_element_type x2 -> x0, local copies, waits for them, and re-layouts: 4.73 us -> none  [expert_grads(): (jnp.einsum('erf,edf->erd', d_gate, w_gate, preferred_element_type=jnp.fl...]
    ppermute x0 -> x3, starting transfers between devices: none -> 3.52 us  [local_step(): lax.ppermute(part[p], 'expert', [(i, i ^ 2 * p) for i in range(GROUP)])]
  transfers between devices with their start and end apart: 6 -> 3, of which waited for: 6 -> 0; matrix products, arithmetic and copies ran while one was open for 32% -> 0% of each run, Pallas kernels for 0% -> 22%
where the time goes in v2:
time: 77 us; the launch traced here: 76.9 us
  Pallas kernels  71.9 us (93%)
  starting transfers between devices  3.52 us (5%)
    pallas_call x1, Pallas kernels, exchange(): pl.pallas_call(exchange_kernel, out_shape=per_layer + per_layer + [pltpu....  55.4 us
    pallas_call x1, Pallas kernels, weight_grads(): pl.pallas_call(weight_grad_kernel, in_specs=[pl.BlockSpec(memory_space=pl...  16.6 us
    ppermute x3, starting transfers between devices, local_step(): lax.ppermute(part[p], 'expert', [(i, i ^ 2 * p) for i in range(GROUP)])  3.52 us
  transfers between devices with their start and end apart: 3, of which 0 were waited for; matrix products, arithmetic and copies ran while one was open for 0% of the time, Pallas kernels for 22%

profile of v2, /device:TPU:0, one launch (start us, length us, event | category | flops | bytes accessed | tf_op | source)
XLA Modules:
  0.0 76.9 jit_solution(13462508414531431388)
XLA Ops:
  0.6 55.4 %shard_map.198 = (bf16[4,192,1024]{2,1,0:T(8,128)(2,1)S(1)}, bf16[4,192,1024]{2,1,0:T(8,128)(2,1)S(1)}, bf16[4,192,512]{2,1,0:T(8,128)(2,1)S(1)}, bf16[4,192,102...) custom-call(bf16[64,1024]{1,0:T(8,128)(2,1)} %y_hbm.1, ...), custom_call_target="tpu_custom_call" | custom-call | flops 10000000000 | bytes 41943040 | tf_op jit(solution)/shard_map/pallas_call | solution.py:279
  56.0 1.2 %collective-permute-start = (f32[64,1024]{1,0:T(8,128)S(1)}, f32[64,1024]{1,0:T(8,128)S(1)}, u32[]{:S(2)}, u32[]{:S(2)}) collective-permute-start(f32[64,1024]{1,0:T(8,128)S(1)} %get-tuple-element.28), channel_id=1, source_target_pairs={{0,2},{1,3},{2,0},{3,1},{4,6},{5,7},{6,4},{7,5},{8,10},{9,11},{10,... | collective-permute-start | bytes 786440 | tf_op jit(solution)/shard_map/ppermute | solution.py:391
  57.2 1.0 %collective-permute-start.1 = (f32[64,1024]{1,0:T(8,128)S(1)}, f32[64,1024]{1,0:T(8,128)S(1)}, u32[]{:S(2)}, u32[]{:S(2)}) collective-permute-start(f32[64,1024]{1,0:T(8,128)S(1)} %get-tuple-element.29), channel_id=1, source_target_pairs={{0,4},{1,5},{2,6},{3,7},{4,0},{5,1},{6,2},{7,3},{8,12},{9,13},{10,... | collective-permute-start | bytes 786440 | tf_op jit(solution)/shard_map/ppermute | solution.py:391
  58.2 1.3 %collective-permute-start.2 = (f32[64,1024]{1,0:T(8,128)S(1)}, f32[64,1024]{1,0:T(8,128)S(1)}, u32[]{:S(2)}, u32[]{:S(2)}) collective-permute-start(f32[64,1024]{1,0:T(8,128)S(1)} %get-tuple-element.30), channel_id=1, source_target_pairs={{0,6},{1,7},{2,4},{3,5},{4,2},{5,3},{6,0},{7,1},{8,14},{9,15},{10,... | collective-permute-start | bytes 786440 | tf_op jit(solution)/shard_map/ppermute | solution.py:391
  59.5 16.6 %shard_map.199 = (f32[4,1024,512]{2,1,0:T(8,128)}, f32[4,1024,512]{2,1,0:T(8,128)}, f32[4,512,1024]{2,1,0:T(8,128)}, f32[4,1024,512]{2,1,0:T(8,128)}, f32[4,1024,512]{2,1,0:T(8,128)}, /*index=5*/f32[4,512,1024]{2,1,0:T(8,128)}) custom-call(bf16[4,192,1024]{2,1,0:T(8,128)(2,1)S(1)} %get-tuple-element.31.u2, bf16[4,192,1024]{2,1,0:T(8,128)(2,1)S(1)} %get-tuple-element.32.z2, ...), custom_call_target="tpu_custom_call" | custom-call | flops 6000000000 | bytes 65011712 | tf_op jit(solution)/shard_map/pallas_call | solution.py:361
  76.1 0.0 collective-permute-done
  76.1 0.0 collective-permute-done.1
  76.1 0.0 collective-permute-done.2
  76.2 0.7 add_convert_fusion
Async XLA Ops:
  56.0 20.1 %collective-permute-start = (f32[64,1024]{1,0:T(8,128)S(1)}, f32[64,1024]{1,0:T(8,128)S(1)}, u32[]{:S(2)}, u32[]{:S(2)}) collective-permute-start(f32[64,1024]{1,0:T(8,128)S(1)} %get-tuple-element.28), channel_id=1, source_target_pairs={{0,2},{1,3},{2,0},{3,1},{4,6},{5,7},{6,4},{7,5},{8,10},{9,11},{10,... | collective-permute-start | bytes 786440 | tf_op jit(solution)/shard_map/ppermute | solution.py:391
  57.2 18.9 %collective-permute-start.1 = (f32[64,1024]{1,0:T(8,128)S(1)}, f32[64,1024]{1,0:T(8,128)S(1)}, u32[]{:S(2)}, u32[]{:S(2)}) collective-permute-start(f32[64,1024]{1,0:T(8,128)S(1)} %get-tuple-element.29), channel_id=1, source_target_pairs={{0,4},{1,5},{2,6},{3,7},{4,0},{5,1},{6,2},{7,3},{8,12},{9,13},{10,... | collective-permute-start | bytes 786440 | tf_op jit(solution)/shard_map/ppermute | solution.py:391
  58.2 17.9 %collective-permute-start.2 = (f32[64,1024]{1,0:T(8,128)S(1)}, f32[64,1024]{1,0:T(8,128)S(1)}, u32[]{:S(2)}, u32[]{:S(2)}) collective-permute-start(f32[64,1024]{1,0:T(8,128)S(1)} %get-tuple-element.30), channel_id=1, source_target_pairs={{0,6},{1,7},{2,4},{3,5},{4,2},{5,3},{6,0},{7,1},{8,14},{9,15},{10,... | collective-permute-start | bytes 786440 | tf_op jit(solution)/shard_map/ppermute | solution.py:391

commit v3 on v2

--- a/solution.py
+++ b/solution.py
@@ -29,7 +29,7 @@
 
 class Copy:
     def __init__(self, copy, log):
-        self.copy, self.log, self.arrived = copy, log, False
+        self.copy, self.log, self.arrived, self.left = copy, log, False, False
 
     def start(self):
         self.copy.start()
@@ -39,10 +39,15 @@
         self.copy.wait_recv()
         self.arrived = True
 
+    def wait_send(self):
+        self.copy.wait_send()
+        self.left = True
+
     def drain(self):
         if not self.arrived:
             self.copy.wait_recv()
-        self.copy.wait_send()
+        if not self.left:
+            self.copy.wait_send()
 
 
 def exchange_kernel(
@@ -80,6 +85,8 @@
         )
     ):
         weights.append(pltpu.make_async_copy(src, dst, w_sem.at[n]))
+    for c in weights[:3]:
+        c.start()
 
     barrier = pltpu.get_barrier_semaphore()
     for dev in (partner,) + devs[1:]:
@@ -99,35 +106,54 @@
     pl.semaphore_wait(barrier, 4)
 
     class Gather:
-        def __init__(self, view, send, recv):
-            self.direct = {p: remote(view(0), view(2 * p), send.at[p], recv.at[2 * p], devs[p]) for p in (3, 1, 2)}
-            self.own = remote(view(0), view(1), send.at[0], recv.at[1], partner)
-            self.passed = {p: remote(view(2 * p), view(2 * p + 1), send.at[3 + p], recv.at[2 * p + 1], partner) for p in (3, 1, 2)}
+        def __init__(self, view, send, recv, relayed=True):
+            def move(src, dst, s, r, dev):
+                return remote(src, dst, send.at[s], recv.at[r], dev)
+
+            half = (pl.ds(0, TOK // 2), pl.ds(TOK // 2, TOK // 2))
+            self.relayed = relayed
+            self.own = move(view(0), view(1), 0, 1, partner)
+            self.direct = [move(view(0), view(2 * p), p, 2 * p, devs[p]) for p in (1, 2)]
+            if relayed:
+                self.cross = [
+                    move(view(2).at[half[0]], view(6).at[half[0]], 3, 6, devs[2]),
+                    move(view(4).at[half[1]], view(6).at[half[1]], 4, 0, devs[1]),
+                ]
+            else:
+                self.cross = [move(view(0), view(6), 3, 6, devs[3])]
+            self.passed = [move(view(2 * p), view(2 * p + 1), 4 + p, 2 * p + 1, partner) for p in (1, 2, 3)]
 
         def launch(self):
-            for c in self.direct.values():
+            for c in self.direct if self.relayed else self.cross + self.direct:
                 c.start()
             self.own.start()
 
-        def forward(self):
-            for p in (1, 2, 3):
+        def relay(self):
+            for p in range(2):
                 self.direct[p].wait_recv()
+                if self.relayed:
+                    self.cross[p].start()
                 self.passed[p].start()
+
+        def last(self):
+            for c in self.cross:
+                c.wait_recv()
+            self.passed[2].start()
 
         def rest(self):
             self.own.wait_recv()
-            for p in (1, 2, 3):
-                self.passed[p].wait_recv()
-
-    routing = Gather(lambda k: route.at[k], r_send, r_recv)
+            for c in self.passed:
+                c.wait_recv()
+
+    routing = Gather(lambda k: route.at[k], r_send, r_recv, relayed=False)
     tokens = [Gather(lambda k, a=a: tok.at[a, k], g_send.at[a], g_recv.at[a]) for a in range(3)]
     routing.launch()
-    for a in range(3):
+    for a in range(2):
         local[a].wait()
         tokens[a].launch()
-    for c in weights:
-        c.start()
-    routing.forward()
+    local[2].wait()
+    routing.relay()
+    routing.last()
     routing.rest()
 
     lane = lax.broadcasted_iota(jnp.int32, (8, 2 * TOK), 1)
@@ -149,7 +175,10 @@
             gate[lay, p] = jnp.broadcast_to(jnp.sum(total, axis=1, keepdims=True), (EXP * PAIR, 128))
 
     build_select(1)
+    tokens[0].relay()
     build_select(0)
+    tokens[1].relay()
+    tokens[2].launch()
 
     def put_rows(dst, p, cols, rows):
         for e in range(EXP):
@@ -181,11 +210,12 @@
         hid[lay][e] = (silu * b).astype(BF)
         dab[lay][e, :, :FFN] = (d_hid * b * sig * (1.0 + a * (1.0 - sig))).astype(BF)
         dab[lay][e, :, FFN:] = (d_hid * silu).astype(BF)
-        rows = dot(dab[lay][e], wcat[lay, e], NT).astype(BF)
-        for p in range(4):
-            dx[p, e] = rows[p * PAIR : (p + 1) * PAIR, :]
 
     def chip_partial(lay, k):
+        for e in range(EXP):
+            rows = dot(dab[lay][e], wcat[lay, e, columns(k), :], NT).astype(BF)
+            for p in range(4):
+                dx[p, e, :, columns(k)] = rows[p * PAIR : (p + 1) * PAIR, :]
         for p in range(4):
             part = dot(selt[lay, p], dx[p, :, :, columns(k)].reshape(EXP * PAIR, KC))
             s_own[lay, k, p] = part[:TOK, :]
@@ -200,32 +230,39 @@
         for k in range(NK)
     ]
 
-    tokens[0].forward()
+    tokens[0].last()
     tokens[0].rest()
     for p in range(4):
         build_u(1, 0, p)
     weights[0].wait()
     weights[1].wait()
     recompute(1)
-    tokens[1].forward()
+    tokens[1].last()
     tokens[1].rest()
     for p in range(4):
         for k in range(NK):
             build_z(1, p, k, tok[1, 2 * p, :, columns(k)], tok[1, 2 * p + 1, :, columns(k)])
+    tokens[2].relay()
     weights[2].wait()
+    for c in weights[3:]:
+        c.start()
     for e in range(EXP):
         expert_rows(1, e, dot(z[1][e], wd[1, e], NT))
-    for k in range(NK):
-        chip_partial(1, k)
-        chip[1][k].start()
-    for k in range(NK):
+    def send_partial(k):
         chip[1][k].wait_recv()
         for p in (3, 1, 2, 0):
             s_own[1, k, p] = s_own[1, k, p] + s_rcv[1, k, p]
         for c in scatter[k]:
             c.start()
 
-    tokens[2].forward()
+    for k in range(NK):
+        chip_partial(1, k)
+        chip[1][k].start()
+        if k:
+            send_partial(k - 1)
+    send_partial(NK - 1)
+
+    tokens[2].last()
     tokens[2].rest()
     for p in range(4):
         build_u(0, 2, p)
@@ -233,7 +270,7 @@
     weights[4].wait()
     recompute(0)
 
-    middle = [Gather(lambda s, k=k: dmid.at[k, s], d_send.at[k], d_recv.at[k]) for k in range(NK)]
+    middle = [Gather(lambda s, k=k: dmid.at[k, s], d_send.at[k], d_recv.at[k], k < RELAYED) for k in range(NK)]
     for k in range(NK):
         for c in scatter[k]:
             c.wait_recv()
@@ -253,19 +290,27 @@
             dh[e] = part if k == 0 else dh[e] + part
 
     for k in range(NK):
-        middle[k].forward()
+        middle[k].relay()
         if k:
-            hidden_grad(k - 1)
+            middle[k - 1].last()
+        if k > 1:
+            hidden_grad(k - 2)
+    middle[NK - 1].last()
+    hidden_grad(NK - 2)
     hidden_grad(NK - 1)
     for e in range(EXP):
         expert_rows(0, e, dh[e])
+    def last_partial(k):
+        chip[0][k].wait_recv()
+        for p in range(4):
+            t1[p][:, columns(k)] = s_own[0, k, p] + s_rcv[0, k, p]
+
     for k in range(NK):
         chip_partial(0, k)
         chip[0][k].start()
-    for k in range(NK):
-        chip[0][k].wait_recv()
-        for p in range(4):
-            t1[p][:, columns(k)] = s_own[0, k, p] + s_rcv[0, k, p]
+        if k:
+            last_partial(k - 1)
+    last_partial(NK - 1)
     for c in sent:
         c.drain()
 
@@ -301,11 +346,11 @@
             pltpu.VMEM((NK, 4, TOK, KC), F32),
             dma((6,)),
             dma((9,)),
-            dma((7,)),
             dma((8,)),
-            dma((3, 7)),
+            dma((8,)),
             dma((3, 8)),
-            dma((NK, 7)),
+            dma((3, 8)),
+            dma((NK, 8)),
             dma((NK, 8)),
             dma((2, NK)),
             dma((2, NK)),
@@ -318,6 +363,7 @@
 
 
 K1_VMEM = 46
+RELAYED = 0
 MB = 256
 SLOTS = 5
 

time: 77 us -> 74.1 us (0.962)
  Pallas kernels: 71.9 us -> 69 us
    pallas_call x1, Pallas kernels: 55.4 us -> 52.5 us  [exchange(): pl.pallas_call(exchange_kernel, out_shape=per_layer + per_layer + [pltpu....]
where the time goes in v3:
time: 74.1 us; the launch traced here: 74 us
  Pallas kernels  69 us (93%)
  starting transfers between devices  3.52 us (5%)
    pallas_call x1, Pallas kernels, exchange(): pl.pallas_call(exchange_kernel, out_shape=per_layer + per_layer + [pltpu....  52.5 us
    pallas_call x1, Pallas kernels, weight_grads(): pl.pallas_call(weight_grad_kernel, in_specs=[pl.BlockSpec(memory_space=pl...  16.6 us
    ppermute x3, starting transfers between devices, local_step(): lax.ppermute(part[p], 'expert', [(i, i ^ 2 * p) for i in range(GROUP)])  3.52 us
  transfers between devices with their start and end apart: 3, of which 0 were waited for; matrix products, arithmetic and copies ran while one was open for 0% of the time, Pallas kernels for 22%

profile of v3, /device:TPU:0, one launch (start us, length us, event | category | flops | bytes accessed | tf_op | source)
XLA Modules:
  0.0 74.0 jit_solution(9722801856667165391)
XLA Ops:
  0.6 52.5 %shard_map.198 = (bf16[4,192,1024]{2,1,0:T(8,128)(2,1)S(1)}, bf16[4,192,1024]{2,1,0:T(8,128)(2,1)S(1)}, bf16[4,192,512]{2,1,0:T(8,128)(2,1)S(1)}, bf16[4,192,102...) custom-call(bf16[64,1024]{1,0:T(8,128)(2,1)} %y_hbm.1, ...), custom_call_target="tpu_custom_call" | custom-call | flops 10000000000 | bytes 41943040 | tf_op jit(solution)/shard_map/pallas_call | solution.py:324
  53.1 1.0 %collective-permute-start = (f32[64,1024]{1,0:T(8,128)S(1)}, f32[64,1024]{1,0:T(8,128)S(1)}, u32[]{:S(2)}, u32[]{:S(2)}) collective-permute-start(f32[64,1024]{1,0:T(8,128)S(1)} %get-tuple-element.28), channel_id=1, source_target_pairs={{0,2},{1,3},{2,0},{3,1},{4,6},{5,7},{6,4},{7,5},{8,10},{9,11},{10,... | collective-permute-start | bytes 786440 | tf_op jit(solution)/shard_map/ppermute | solution.py:437
  54.1 1.1 %collective-permute-start.1 = (f32[64,1024]{1,0:T(8,128)S(1)}, f32[64,1024]{1,0:T(8,128)S(1)}, u32[]{:S(2)}, u32[]{:S(2)}) collective-permute-start(f32[64,1024]{1,0:T(8,128)S(1)} %get-tuple-element.29), channel_id=1, source_target_pairs={{0,4},{1,5},{2,6},{3,7},{4,0},{5,1},{6,2},{7,3},{8,12},{9,13},{10,... | collective-permute-start | bytes 786440 | tf_op jit(solution)/shard_map/ppermute | solution.py:437
  55.3 1.4 %collective-permute-start.2 = (f32[64,1024]{1,0:T(8,128)S(1)}, f32[64,1024]{1,0:T(8,128)S(1)}, u32[]{:S(2)}, u32[]{:S(2)}) collective-permute-start(f32[64,1024]{1,0:T(8,128)S(1)} %get-tuple-element.30), channel_id=1, source_target_pairs={{0,6},{1,7},{2,4},{3,5},{4,2},{5,3},{6,0},{7,1},{8,14},{9,15},{10,... | collective-permute-start | bytes 786440 | tf_op jit(solution)/shard_map/ppermute | solution.py:437
  56.6 16.6 %shard_map.199 = (f32[4,1024,512]{2,1,0:T(8,128)}, f32[4,1024,512]{2,1,0:T(8,128)}, f32[4,512,1024]{2,1,0:T(8,128)}, f32[4,1024,512]{2,1,0:T(8,128)}, f32[4,1024,512]{2,1,0:T(8,128)}, /*index=5*/f32[4,512,1024]{2,1,0:T(8,128)}) custom-call(bf16[4,192,1024]{2,1,0:T(8,128)(2,1)S(1)} %get-tuple-element.31.u2, bf16[4,192,1024]{2,1,0:T(8,128)(2,1)S(1)} %get-tuple-element.32.z2, ...), custom_call_target="tpu_custom_call" | custom-call | flops 6000000000 | bytes 65011712 | tf_op jit(solution)/shard_map/pallas_call | solution.py:407
  73.2 0.0 collective-permute-done
  73.2 0.0 collective-permute-done.1
  73.2 0.0 collective-permute-done.2
  73.3 0.7 add_convert_fusion
Async XLA Ops:
  53.1 20.1 %collective-permute-start = (f32[64,1024]{1,0:T(8,128)S(1)}, f32[64,1024]{1,0:T(8,128)S(1)}, u32[]{:S(2)}, u32[]{:S(2)}) collective-permute-start(f32[64,1024]{1,0:T(8,128)S(1)} %get-tuple-element.28), channel_id=1, source_target_pairs={{0,2},{1,3},{2,0},{3,1},{4,6},{5,7},{6,4},{7,5},{8,10},{9,11},{10,... | collective-permute-start | bytes 786440 | tf_op jit(solution)/shard_map/ppermute | solution.py:437
  54.1 19.1 %collective-permute-start.1 = (f32[64,1024]{1,0:T(8,128)S(1)}, f32[64,1024]{1,0:T(8,128)S(1)}, u32[]{:S(2)}, u32[]{:S(2)}) collective-permute-start(f32[64,1024]{1,0:T(8,128)S(1)} %get-tuple-element.29), channel_id=1, source_target_pairs={{0,4},{1,5},{2,6},{3,7},{4,0},{5,1},{6,2},{7,3},{8,12},{9,13},{10,... | collective-permute-start | bytes 786440 | tf_op jit(solution)/shard_map/ppermute | solution.py:437
  55.3 18.0 %collective-permute-start.2 = (f32[64,1024]{1,0:T(8,128)S(1)}, f32[64,1024]{1,0:T(8,128)S(1)}, u32[]{:S(2)}, u32[]{:S(2)}) collective-permute-start(f32[64,1024]{1,0:T(8,128)S(1)} %get-tuple-element.30), channel_id=1, source_target_pairs={{0,6},{1,7},{2,4},{3,5},{4,2},{5,3},{6,0},{7,1},{8,14},{9,15},{10,... | collective-permute-start | bytes 786440 | tf_op jit(solution)/shard_map/ppermute | solution.py:437

commit v4 on v3

--- a/solution.py
+++ b/solution.py
@@ -19,7 +19,6 @@
 KC = DIM // NK
 BF = jnp.bfloat16
 F32 = jnp.float32
-NT = (((1,), (1,)), ((), ()))
 TN = (((0,), (0,)), ((), ()))
 
 
@@ -53,7 +52,7 @@
 def exchange_kernel(
     y_hbm, dy_hbm, x_hbm, e2, g2, s2, e1, g1, s1, wg2, wu2, wd2, wg1, wu1, wd1,
     u2, z2, hid2, dab2, u1, z1, hid1, dab1, t1a, t1b, t1c, t1d, dym,
-    wcat, wd, tok, dmid, raw_int, raw_gate, route, sel, selt, gate, act, dh, dx, s_oth, s_rcv, s_own, rs_rcv,
+    wcat, wd, wcat_t, wd_t, tok, dmid, raw_int, raw_gate, route, sel, selt, gate, act, dh, dx, s_oth, s_rcv, s_own, rs_rcv,
     w_sem, l_sem, r_send, r_recv, g_send, g_recv, d_send, d_recv, c_send, c_recv, p_send, p_recv,
 ):
     me = lax.axis_index("expert")
@@ -80,8 +79,8 @@
     weights = []
     for n, (src, dst) in enumerate(
         (
-            (wg2, wcat.at[1, :, :, left]), (wu2, wcat.at[1, :, :, right]), (wd2, wd.at[1]),
-            (wg1, wcat.at[0, :, :, left]), (wu1, wcat.at[0, :, :, right]), (wd1, wd.at[0]),
+            (wg2, wcat.at[:, :, left]), (wu2, wcat.at[:, :, right]), (wd2, wd),
+            (wg1, wcat.at[:, :, left]), (wu1, wcat.at[:, :, right]), (wd1, wd),
         )
     ):
         weights.append(pltpu.make_async_copy(src, dst, w_sem.at[n]))
@@ -145,6 +144,14 @@
             for c in self.passed:
                 c.wait_recv()
 
+    def transpose_weights():
+        for e in range(EXP):
+            for i in range(DIM // TR):
+                for j in range(2 * FFN // TR):
+                    wcat_t[e, j * TR : (j + 1) * TR, i * TR : (i + 1) * TR] = wcat[e, i * TR : (i + 1) * TR, j * TR : (j + 1) * TR].T
+                for j in range(FFN // TR):
+                    wd_t[e, i * TR : (i + 1) * TR, j * TR : (j + 1) * TR] = wd[e, j * TR : (j + 1) * TR, i * TR : (i + 1) * TR].T
+
     routing = Gather(lambda k: route.at[k], r_send, r_recv, relayed=False)
     tokens = [Gather(lambda k, a=a: tok.at[a, k], g_send.at[a], g_recv.at[a]) for a in range(3)]
     routing.launch()
@@ -152,6 +159,9 @@
         local[a].wait()
         tokens[a].launch()
     local[2].wait()
+    for c in weights[:3]:
+        c.wait()
+    transpose_weights()
     routing.relay()
     routing.last()
     routing.rest()
@@ -200,7 +210,7 @@
 
     def recompute(lay):
         for e in range(EXP):
-            act[e] = dot(u[lay][e], wcat[lay, e]).astype(BF)
+            act[e] = dot(u[lay][e], wcat[e]).astype(BF)
 
     def expert_rows(lay, e, d_hid):
         a = act[e, :, :FFN].astype(F32)
@@ -213,7 +223,7 @@
 
     def chip_partial(lay, k):
         for e in range(EXP):
-            rows = dot(dab[lay][e], wcat[lay, e, columns(k), :], NT).astype(BF)
+            rows = dot(dab[lay][e], wcat_t[e, :, columns(k)]).astype(BF)
             for p in range(4):
                 dx[p, e, :, columns(k)] = rows[p * PAIR : (p + 1) * PAIR, :]
         for p in range(4):
@@ -225,29 +235,35 @@
         [remote(s_oth.at[lay, k], s_rcv.at[lay, k], c_send.at[lay, k], c_recv.at[lay, k], partner) for k in range(NK)]
         for lay in range(2)
     ]
-    scatter = [
-        [remote(s_own.at[1, k, p], rs_rcv.at[k, p], p_send.at[k, p], p_recv.at[k, p], devs[p]) for p in (3, 1, 2)]
-        for k in range(NK)
-    ]
+    first = [1 + k % 2 for k in range(NK)]
+
+    def toward(k, p, slot, dev):
+        return remote(s_own.at[1, k, p], rs_rcv.at[k, slot], p_send.at[k, slot], p_recv.at[k, slot], devs[dev])
+
+    scatter = [[toward(k, 3, 1, first[k]), toward(k, first[k], 0, first[k])] for k in range(NK)]
+    onward = [toward(k, 3 - first[k], 2, 3 - first[k]) for k in range(NK)]
+
+    def relay_partial(k):
+        scatter[k][0].wait_recv()
+        p = 3 - first[k]
+        s_own[1, k, p] = s_own[1, k, p] + rs_rcv[k, 1]
+        onward[k].start()
 
     tokens[0].last()
     tokens[0].rest()
     for p in range(4):
         build_u(1, 0, p)
-    weights[0].wait()
-    weights[1].wait()
     recompute(1)
+    for c in weights[3:]:
+        c.start()
     tokens[1].last()
     tokens[1].rest()
     for p in range(4):
         for k in range(NK):
             build_z(1, p, k, tok[1, 2 * p, :, columns(k)], tok[1, 2 * p + 1, :, columns(k)])
     tokens[2].relay()
-    weights[2].wait()
-    for c in weights[3:]:
-        c.start()
     for e in range(EXP):
-        expert_rows(1, e, dot(z[1][e], wd[1, e], NT))
+        expert_rows(1, e, dot(z[1][e], wd_t[e]))
     def send_partial(k):
         chip[1][k].wait_recv()
         for p in (3, 1, 2, 0):
@@ -262,31 +278,35 @@
             send_partial(k - 1)
     send_partial(NK - 1)
 
+    relay_partial(0)
+    relay_partial(1)
     tokens[2].last()
     tokens[2].rest()
     for p in range(4):
         build_u(0, 2, p)
-    weights[3].wait()
-    weights[4].wait()
+    for c in weights[3:]:
+        c.wait()
+    relay_partial(2)
+    relay_partial(3)
     recompute(0)
 
     middle = [Gather(lambda s, k=k: dmid.at[k, s], d_send.at[k], d_recv.at[k], k < RELAYED) for k in range(NK)]
     for k in range(NK):
-        for c in scatter[k]:
-            c.wait_recv()
-        total = s_own[1, k, 0] + rs_rcv[k, 1] + rs_rcv[k, 2] + rs_rcv[k, 3]
+        scatter[k][1].wait_recv()
+        onward[k].wait_recv()
+        total = s_own[1, k, 0] + rs_rcv[k, 0] + rs_rcv[k, 2]
         new = (tok[1, 0, :, columns(k)].astype(F32) + total).astype(BF)
         dmid[k, 0] = new
         dym[:, columns(k)] = new
         middle[k].launch()
-    weights[5].wait()
+    transpose_weights()
 
     def hidden_grad(k):
         middle[k].rest()
         for p in range(4):
             build_z(0, p, k, dmid[k, 2 * p], dmid[k, 2 * p + 1])
         for e in range(EXP):
-            part = dot(z[0][e, :, columns(k)], wd[0, e, :, columns(k)], NT)
+            part = dot(z[0][e, :, columns(k)], wd_t[e, columns(k), :])
             dh[e] = part if k == 0 else dh[e] + part
 
     for k in range(NK):
@@ -327,8 +347,10 @@
         in_specs=[hbm_spec] * 15,
         out_specs=[vmem_spec] * 13,
         scratch_shapes=[
-            pltpu.VMEM((2, EXP, DIM, 2 * FFN), BF),
-            pltpu.VMEM((2, EXP, FFN, DIM), BF),
+            pltpu.VMEM((EXP, DIM, 2 * FFN), BF),
+            pltpu.VMEM((EXP, FFN, DIM), BF),
+            pltpu.VMEM((EXP, 2 * FFN, DIM), BF),
+            pltpu.VMEM((EXP, DIM, FFN), BF),
             pltpu.VMEM((3, GROUP, TOK, DIM), BF),
             pltpu.VMEM((NK, GROUP, TOK, KC), BF),
             pltpu.VMEM((4, 8, TOK), jnp.int32),
@@ -364,6 +386,7 @@
 
 K1_VMEM = 46
 RELAYED = 0
+TR = 256
 MB = 256
 SLOTS = 5
 

time: 74.1 us -> 72.1 us (0.973)
  Pallas kernels: 69 us -> 67 us
    pallas_call x1, Pallas kernels: 52.5 us -> 50.4 us  [exchange(): pl.pallas_call(exchange_kernel, out_shape=per_layer + per_layer + [pltpu....]
  transfers between devices with their start and end apart: 3 -> 3, of which waited for: 0 -> 0; matrix products, arithmetic and copies ran while one was open for 0% -> 0% of each run, Pallas kernels for 22% -> 23%
where the time goes in v4:
time: 72.1 us; the launch traced here: 72 us
  Pallas kernels  67 us (93%)
  starting transfers between devices  3.52 us (5%)
  other arithmetic  0.73 us (1%)
    pallas_call x1, Pallas kernels, exchange(): pl.pallas_call(exchange_kernel, out_shape=per_layer + per_layer + [pltpu....  50.4 us
    pallas_call x1, Pallas kernels, weight_grads(): pl.pallas_call(weight_grad_kernel, in_specs=[pl.BlockSpec(memory_space=pl...  16.6 us
    ppermute x3, starting transfers between devices, local_step(): lax.ppermute(part[p], 'expert', [(i, i ^ 2 * p) for i in range(GROUP)])  3.52 us
  transfers between devices with their start and end apart: 3, of which 0 were waited for; matrix products, arithmetic and copies ran while one was open for 0% of the time, Pallas kernels for 23%

profile of v4, /device:TPU:0, one launch (start us, length us, event | category | flops | bytes accessed | tf_op | source)
XLA Modules:
  0.0 72.0 jit_solution(4199528434896313305)
XLA Ops:
  0.6 50.4 %shard_map.198 = (bf16[4,192,1024]{2,1,0:T(8,128)(2,1)S(1)}, bf16[4,192,1024]{2,1,0:T(8,128)(2,1)S(1)}, bf16[4,192,512]{2,1,0:T(8,128)(2,1)S(1)}, bf16[4,192,102...) custom-call(bf16[64,1024]{1,0:T(8,128)(2,1)} %y_hbm.1, ...), custom_call_target="tpu_custom_call" | custom-call | flops 10000000000 | bytes 41943040 | tf_op jit(solution)/shard_map/pallas_call | solution.py:344
  51.1 1.8 %collective-permute-start = (f32[64,1024]{1,0:T(8,128)S(1)}, f32[64,1024]{1,0:T(8,128)S(1)}, u32[]{:S(2)}, u32[]{:S(2)}) collective-permute-start(f32[64,1024]{1,0:T(8,128)S(1)} %get-tuple-element.28), channel_id=1, source_target_pairs={{0,2},{1,3},{2,0},{3,1},{4,6},{5,7},{6,4},{7,5},{8,10},{9,11},{10,... | collective-permute-start | bytes 786440 | tf_op jit(solution)/shard_map/ppermute | solution.py:460
  52.9 0.2 collective-permute-start.1
  53.1 1.5 %collective-permute-start.2 = (f32[64,1024]{1,0:T(8,128)S(1)}, f32[64,1024]{1,0:T(8,128)S(1)}, u32[]{:S(2)}, u32[]{:S(2)}) collective-permute-start(f32[64,1024]{1,0:T(8,128)S(1)} %get-tuple-element.30), channel_id=1, source_target_pairs={{0,6},{1,7},{2,4},{3,5},{4,2},{5,3},{6,0},{7,1},{8,14},{9,15},{10,... | collective-permute-start | bytes 786440 | tf_op jit(solution)/shard_map/ppermute | solution.py:460
  54.6 16.6 %shard_map.199 = (f32[4,1024,512]{2,1,0:T(8,128)}, f32[4,1024,512]{2,1,0:T(8,128)}, f32[4,512,1024]{2,1,0:T(8,128)}, f32[4,1024,512]{2,1,0:T(8,128)}, f32[4,1024,512]{2,1,0:T(8,128)}, /*index=5*/f32[4,512,1024]{2,1,0:T(8,128)}) custom-call(bf16[4,192,1024]{2,1,0:T(8,128)(2,1)S(1)} %get-tuple-element.31.u2, bf16[4,192,1024]{2,1,0:T(8,128)(2,1)S(1)} %get-tuple-element.32.z2, ...), custom_call_target="tpu_custom_call" | custom-call | flops 6000000000 | bytes 65011712 | tf_op jit(solution)/shard_map/pallas_call | solution.py:430
  71.2 0.0 collective-permute-done
  71.2 0.0 collective-permute-done.1
  71.2 0.0 collective-permute-done.2
  71.2 0.7 %add_convert_fusion = bf16[64,1024]{1,0:T(8,128)(2,1)} fusion(f32[64,1024]{1,0:T(8,128)S(1)} %collective-permute-done.2, f32[64,1024]{1,0:T(8,128)S(1)} %collective-permute-done.1, f32[64,1024]{1,0:T(8,128)S(1)} %get-tuple-element.27, f32[64,1024]{1,0:T(8,128)S(1)} %collective-permute-done, bf16[64,1024]{1,0:T(8,128)(2,1)S(1)} %get-tuple-element.26), kind=kLoop, calls=%fused_computation | loop fusion | flops 393216 | bytes 1310720 | tf_op jit(solution)/shard_map/convert_element_type | solution.py:463
Async XLA Ops:
  51.1 20.1 %collective-permute-start = (f32[64,1024]{1,0:T(8,128)S(1)}, f32[64,1024]{1,0:T(8,128)S(1)}, u32[]{:S(2)}, u32[]{:S(2)}) collective-permute-start(f32[64,1024]{1,0:T(8,128)S(1)} %get-tuple-element.28), channel_id=1, source_target_pairs={{0,2},{1,3},{2,0},{3,1},{4,6},{5,7},{6,4},{7,5},{8,10},{9,11},{10,... | collective-permute-start | bytes 786440 | tf_op jit(solution)/shard_map/ppermute | solution.py:460
  52.9 18.3 %collective-permute-start.1 = (f32[64,1024]{1,0:T(8,128)S(1)}, f32[64,1024]{1,0:T(8,128)S(1)}, u32[]{:S(2)}, u32[]{:S(2)}) collective-permute-start(f32[64,1024]{1,0:T(8,128)S(1)} %get-tuple-element.29), channel_id=1, source_target_pairs={{0,4},{1,5},{2,6},{3,7},{4,0},{5,1},{6,2},{7,3},{8,12},{9,13},{10,... | collective-permute-start | bytes 786440 | tf_op jit(solution)/shard_map/ppermute | solution.py:460
  53.1 18.1 %collective-permute-start.2 = (f32[64,1024]{1,0:T(8,128)S(1)}, f32[64,1024]{1,0:T(8,128)S(1)}, u32[]{:S(2)}, u32[]{:S(2)}) collective-permute-start(f32[64,1024]{1,0:T(8,128)S(1)} %get-tuple-element.30), channel_id=1, source_target_pairs={{0,6},{1,7},{2,4},{3,5},{4,2},{5,3},{6,0},{7,1},{8,14},{9,15},{10,... | collective-permute-start | bytes 786440 | tf_op jit(solution)/shard_map/ppermute | solution.py:460

commit v5 on v4

--- a/solution.py
+++ b/solution.py
@@ -189,6 +189,7 @@
     build_select(0)
     tokens[1].relay()
     tokens[2].launch()
+    tokens[0].last()
 
     def put_rows(dst, p, cols, rows):
         for e in range(EXP):
@@ -249,7 +250,6 @@
         s_own[1, k, p] = s_own[1, k, p] + rs_rcv[k, 1]
         onward[k].start()
 
-    tokens[0].last()
     tokens[0].rest()
     for p in range(4):
         build_u(1, 0, p)
@@ -257,11 +257,11 @@
     for c in weights[3:]:
         c.start()
     tokens[1].last()
+    tokens[2].relay()
     tokens[1].rest()
     for p in range(4):
         for k in range(NK):
             build_z(1, p, k, tok[1, 2 * p, :, columns(k)], tok[1, 2 * p + 1, :, columns(k)])
-    tokens[2].relay()
     for e in range(EXP):
         expert_rows(1, e, dot(z[1][e], wd_t[e]))
     def send_partial(k):
@@ -307,7 +307,10 @@
             build_z(0, p, k, dmid[k, 2 * p], dmid[k, 2 * p + 1])
         for e in range(EXP):
             part = dot(z[0][e, :, columns(k)], wd_t[e, columns(k), :])
-            dh[e] = part if k == 0 else dh[e] + part
+            if k == NK - 1:
+                expert_rows(0, e, dh[e] + part)
+            else:
+                dh[e] = part if k == 0 else dh[e] + part
 
     for k in range(NK):
         middle[k].relay()
@@ -318,8 +321,6 @@
     middle[NK - 1].last()
     hidden_grad(NK - 2)
     hidden_grad(NK - 1)
-    for e in range(EXP):
-        expert_rows(0, e, dh[e])
     def last_partial(k):
         chip[0][k].wait_recv()
         for p in range(4):
@@ -387,7 +388,7 @@
 K1_VMEM = 46
 RELAYED = 0
 TR = 256
-MB = 256
+MB = 512
 SLOTS = 5
 
 

time: 72.1 us -> 71.6 us (level)
  no operation moved by 1% of the time
where the time goes in v5:
time: 71.6 us; the launch traced here: 71.5 us
  Pallas kernels  66.5 us (93%)
  starting transfers between devices  3.52 us (5%)
  other arithmetic  0.73 us (1%)
    pallas_call x1, Pallas kernels, exchange(): pl.pallas_call(exchange_kernel, out_shape=per_layer + per_layer + [pltpu....  50 us
    pallas_call x1, Pallas kernels, weight_grads(): pl.pallas_call(weight_grad_kernel, in_specs=[pl.BlockSpec(memory_space=pl...  16.5 us
    ppermute x3, starting transfers between devices, local_step(): lax.ppermute(part[p], 'expert', [(i, i ^ 2 * p) for i in range(GROUP)])  3.52 us
  transfers between devices with their start and end apart: 3, of which 0 were waited for; matrix products, arithmetic and copies ran while one was open for 0% of the time, Pallas kernels for 23%

profile of v5, /device:TPU:0, one launch (start us, length us, event | category | flops | bytes accessed | tf_op | source)
XLA Modules:
  0.0 71.5 jit_solution(11658555924638500250)
XLA Ops:
  0.6 50.0 %shard_map.198 = (bf16[4,192,1024]{2,1,0:T(8,128)(2,1)S(1)}, bf16[4,192,1024]{2,1,0:T(8,128)(2,1)S(1)}, bf16[4,192,512]{2,1,0:T(8,128)(2,1)S(1)}, bf16[4,192,102...) custom-call(bf16[64,1024]{1,0:T(8,128)(2,1)} %y_hbm.1, ...), custom_call_target="tpu_custom_call" | custom-call | flops 10000000000 | bytes 41943040 | tf_op jit(solution)/shard_map/pallas_call | solution.py:345
  50.7 1.8 %collective-permute-start = (f32[64,1024]{1,0:T(8,128)S(1)}, f32[64,1024]{1,0:T(8,128)S(1)}, u32[]{:S(2)}, u32[]{:S(2)}) collective-permute-start(f32[64,1024]{1,0:T(8,128)S(1)} %get-tuple-element.28), channel_id=1, source_target_pairs={{0,2},{1,3},{2,0},{3,1},{4,6},{5,7},{6,4},{7,5},{8,10},{9,11},{10,... | collective-permute-start | bytes 786440 | tf_op jit(solution)/shard_map/ppermute | solution.py:461
  52.5 0.2 collective-permute-start.1
  52.7 1.5 %collective-permute-start.2 = (f32[64,1024]{1,0:T(8,128)S(1)}, f32[64,1024]{1,0:T(8,128)S(1)}, u32[]{:S(2)}, u32[]{:S(2)}) collective-permute-start(f32[64,1024]{1,0:T(8,128)S(1)} %get-tuple-element.30), channel_id=1, source_target_pairs={{0,6},{1,7},{2,4},{3,5},{4,2},{5,3},{6,0},{7,1},{8,14},{9,15},{10,... | collective-permute-start | bytes 786440 | tf_op jit(solution)/shard_map/ppermute | solution.py:461
  54.2 16.5 %shard_map.199 = (f32[4,1024,512]{2,1,0:T(8,128)}, f32[4,1024,512]{2,1,0:T(8,128)}, f32[4,512,1024]{2,1,0:T(8,128)}, f32[4,1024,512]{2,1,0:T(8,128)}, f32[4,1024,512]{2,1,0:T(8,128)}, /*index=5*/f32[4,512,1024]{2,1,0:T(8,128)}) custom-call(bf16[4,192,1024]{2,1,0:T(8,128)(2,1)S(1)} %get-tuple-element.31.u2, bf16[4,192,1024]{2,1,0:T(8,128)(2,1)S(1)} %get-tuple-element.32.z2, ...), custom_call_target="tpu_custom_call" | custom-call | flops 6000000000 | bytes 65011712 | tf_op jit(solution)/shard_map/pallas_call | solution.py:431
  70.7 0.0 collective-permute-done
  70.7 0.0 collective-permute-done.1
  70.7 0.0 collective-permute-done.2
  70.7 0.7 %add_convert_fusion = bf16[64,1024]{1,0:T(8,128)(2,1)} fusion(f32[64,1024]{1,0:T(8,128)S(1)} %collective-permute-done.2, f32[64,1024]{1,0:T(8,128)S(1)} %collective-permute-done.1, f32[64,1024]{1,0:T(8,128)S(1)} %get-tuple-element.27, f32[64,1024]{1,0:T(8,128)S(1)} %collective-permute-done, bf16[64,1024]{1,0:T(8,128)(2,1)S(1)} %get-tuple-element.26), kind=kLoop, calls=%fused_computation | loop fusion | flops 393216 | bytes 1310720 | tf_op jit(solution)/shard_map/convert_element_type | solution.py:464
Async XLA Ops:
  50.7 20.0 %collective-permute-start = (f32[64,1024]{1,0:T(8,128)S(1)}, f32[64,1024]{1,0:T(8,128)S(1)}, u32[]{:S(2)}, u32[]{:S(2)}) collective-permute-start(f32[64,1024]{1,0:T(8,128)S(1)} %get-tuple-element.28), channel_id=1, source_target_pairs={{0,2},{1,3},{2,0},{3,1},{4,6},{5,7},{6,4},{7,5},{8,10},{9,11},{10,... | collective-permute-start | bytes 786440 | tf_op jit(solution)/shard_map/ppermute | solution.py:461
  52.5 18.2 %collective-permute-start.1 = (f32[64,1024]{1,0:T(8,128)S(1)}, f32[64,1024]{1,0:T(8,128)S(1)}, u32[]{:S(2)}, u32[]{:S(2)}) collective-permute-start(f32[64,1024]{1,0:T(8,128)S(1)} %get-tuple-element.29), channel_id=1, source_target_pairs={{0,4},{1,5},{2,6},{3,7},{4,0},{5,1},{6,2},{7,3},{8,12},{9,13},{10,... | collective-permute-start | bytes 786440 | tf_op jit(solution)/shard_map/ppermute | solution.py:461
  52.7 18.0 %collective-permute-start.2 = (f32[64,1024]{1,0:T(8,128)S(1)}, f32[64,1024]{1,0:T(8,128)S(1)}, u32[]{:S(2)}, u32[]{:S(2)}) collective-permute-start(f32[64,1024]{1,0:T(8,128)S(1)} %get-tuple-element.30), channel_id=1, source_target_pairs={{0,6},{1,7},{2,4},{3,5},{4,2},{5,3},{6,0},{7,1},{8,14},{9,15},{10,... | collective-permute-start | bytes 786440 | tf_op jit(solution)/shard_map/ppermute | solution.py:461
